TPU v7x, 32 devices: a 4x2x2 block of a 4x4x8 slice. The times are simulated.
32 devices in a mesh: dp: 4 (over y, z), ep: 8 (over x, core).
Axes of the slice: x: 4, y: 2, z: 2, core: 2. Of those that a mesh axis runs over, the one named last changes fastest.
The devices are a block of a 4x4x8 slice.
Arguments:
- x_a: bfloat16 [8192, 2048], P(('dp', 'ep')), parts along dimension 0
- route_a: int32 [8192, 6], P(('dp', 'ep')), parts along dimension 0
- gate_a: float32 [8192, 6], P(('dp', 'ep')), parts along dimension 0
- h_b: bfloat16 [8192, 2048], P(('dp', 'ep')), parts along dimension 0
- attn_b: bfloat16 [8192, 2048], P(('dp', 'ep')), parts along dimension 0
- route_b: int32 [8192, 6], P(('dp', 'ep')), parts along dimension 0
- gate_b: float32 [8192, 6], P(('dp', 'ep')), parts along dimension 0
- w_qkv: bfloat16 [2048, 6144], replicated
- w_o: bfloat16 [2048, 2048], replicated
- w_gate: bfloat16 [64, 2048, 1408], P('ep')
- w_up: bfloat16 [64, 2048, 1408], P('ep')
- w_down: bfloat16 [64, 1408, 2048], P('ep')
Outputs:
- output 1: bfloat16 [8192, 2048], P(('dp', 'ep')), parts along dimension 0
- output 2: bfloat16 [8192, 2048], P(('dp', 'ep')), parts along dimension 0
- output 3: bfloat16 [8192, 6144], P(('dp', 'ep')), parts along dimension 0
There are 4 independent parts. A program takes and returns all parts, laid end to end along the dimension named above; an argument that names none is the same for every part.
All inputs are finite; a program needn't handle non-finite values.
Results may differ from a plain program's by a relative error of at most 0.011069.
Values are sent between devices in bfloat16 or wider.
A program may use at most 768 MiB of HBM per device.

v0:
```python
import jax
import jax.numpy as jnp
from jax import lax
from jax.sharding import PartitionSpec as P


def route_slots(route_ids, n_experts, n_devs, capacity):
    tok_n, top_k = route_ids.shape
    local_n = n_experts // n_devs
    flat_route = route_ids.reshape(tok_n * top_k)
    one_hot = (flat_route[:, None] == jnp.arange(n_experts)[None, :]).astype(jnp.int32)
    slot_rank = jnp.sum((jnp.cumsum(one_hot, axis=0) - 1) * one_hot, axis=1)
    owner = flat_route // local_n
    local_id = flat_route % local_n
    slot_ids = local_id * (n_devs * capacity) + owner * capacity + slot_rank
    return slot_ids.reshape(tok_n, top_k)


def expert_ffn(rows_in, w_gate, w_up, w_down):
    gate_act = jnp.einsum('erd,edf->erf', rows_in, w_gate, preferred_element_type=jnp.float32)
    up_act = jnp.einsum('erd,edf->erf', rows_in, w_up, preferred_element_type=jnp.float32)
    hidden = (jax.nn.silu(gate_act) * up_act).astype(jnp.bfloat16)
    return jnp.einsum('erf,efd->erd', hidden, w_down, preferred_element_type=jnp.float32).astype(jnp.bfloat16)


def moe_local(tokens, route_ids, gate_vals, w_gate, w_up, w_down, n_devs):
    tok_n, model_dim = tokens.shape
    top_k = route_ids.shape[1]
    local_n = w_gate.shape[0]
    n_experts = local_n * n_devs
    capacity = min(tok_n, 2 * ((tok_n * top_k + n_experts - 1) // n_experts))
    n_slots = n_experts * capacity
    slot_ids = route_slots(route_ids, n_experts, n_devs, capacity)
    picker = (slot_ids[:, :, None] == jnp.arange(n_slots)[None, None, :]).astype(jnp.bfloat16)
    placer = jnp.sum(picker, axis=1)
    send_buf = jnp.einsum('ts,td->sd', placer, tokens, preferred_element_type=jnp.float32).astype(jnp.bfloat16)
    send_buf = send_buf.reshape(local_n, n_devs, capacity, model_dim)
    recv_buf = lax.all_to_all(send_buf, 'ep', 1, 1, tiled=True)
    expert_out = expert_ffn(recv_buf.reshape(local_n, n_devs * capacity, model_dim), w_gate, w_up, w_down)
    back_buf = lax.all_to_all(expert_out.reshape(local_n, n_devs, capacity, model_dim), 'ep', 1, 1, tiled=True)
    picked = jnp.einsum('tjs,sd->tjd', picker, back_buf.reshape(n_slots, model_dim), preferred_element_type=jnp.float32)
    mixture = jnp.zeros((tok_n, model_dim), jnp.float32)
    for choice in range(top_k):
        mixture = mixture + gate_vals[:, choice:choice + 1] * picked[:, choice]
    return (tokens.astype(jnp.float32) + mixture).astype(jnp.bfloat16)


def solution(mesh):
    n_devs = mesh.shape['ep']

    def local_step(x_a, route_a, gate_a, h_b, attn_b, route_b, gate_b, w_qkv, w_o, w_gate, w_up, w_down):
        out_a = moe_local(x_a, route_a, gate_a, w_gate, w_up, w_down, n_devs)
        qkv_b = jnp.dot(h_b, w_qkv, preferred_element_type=jnp.float32).astype(jnp.bfloat16)
        proj_b = jnp.dot(attn_b, w_o, preferred_element_type=jnp.float32).astype(jnp.bfloat16)
        mid_b = (h_b.astype(jnp.float32) + proj_b.astype(jnp.float32)).astype(jnp.bfloat16)
        out_b = moe_local(mid_b, route_b, gate_b, w_gate, w_up, w_down, n_devs)
        return out_a, out_b, qkv_b

    row_spec = P(('dp', 'ep'), None)
    full_spec = P(None, None)
    expert_spec = P('ep', None, None)
    return jax.shard_map(
        local_step,
        mesh=mesh,
        in_specs=(row_spec, row_spec, row_spec, row_spec, row_spec, row_spec, row_spec, full_spec, full_spec, expert_spec, expert_spec, expert_spec),
        out_specs=(row_spec, row_spec, row_spec),
        check_vma=False,
    )
```

profile of v0, /device:TPU:81, one launch (start us, length us, event | category | flops | bytes accessed | tf_op | source)
XLA Modules:
  0.0 664.9 jit_solution(14553404691989652683)
XLA Ops:
  0.6 0.0 copy-start
  0.6 0.9 copy.68
  1.6 0.1 eq.94
  1.7 0.1 eq.90
  1.9 18.1 %reduce-window.16 = s32[64,12,128]{2,1,0:T(8,128)S(1)} reduce-window(s32[64,12,128]{2,1,0:T(8,128)S(1)} %fusion.38, s32[]{:T(128)} %constant.52.clone.1), window={size=1x1x128 pad=0_0x0_0x127_0}, to_apply=%region_4.5 | reduce-window | flops 12484608 | bytes 786436 | tf_op jit(solution)/shard_map/reduce-window.2
  20.0 0.2 slice.120
  20.2 0.3 copy.70
  20.5 0.1 copy.71
  20.6 0.2 add_add_fusion
  20.8 0.1 fusion.40
  21.0 0.1 reduce_sum.50
  21.1 0.1 copy.72
  21.2 0.7 fusion.49
  21.9 0.0 copy-start.5
  22.0 2.9 fusion.5
  24.9 0.0 copy-done.5
  24.9 0.0 copy-done
  24.9 6.9 %fusion.10 = bf16[256,2048]{1,0:T(8,128)(2,1)} fusion(bf16[256,2048]{1,0:T(8,128)(2,1)S(1)} %copy-done, bf16[2048,2048]{1,0:T(8,128)(2,1)} %param.20, bf16[256,2048]{1,0:T(8,128)(2,1)} %param.15), kind=kOutput, calls=%fused_computation.20 | convolution fusion | flops 2150105088 | bytes 11534336 | tf_op jit(solution)/shard_map/dot_general | solution.py:54
  31.8 4.9 convolution_convert_fusion
  36.8 5.5 copy.73
  42.3 8.1 %all-to-all-start.2 = ((bf16[8,8,48,2048]{3,2,0,1:T(8,128)(2,1)}), bf16[8,8,48,2048]{3,2,0,1:T(8,128)(2,1)}, u32[]{:S(2)}, u32[]{:S(2)}) async-start(bf16[8,8,48,2048]{3,2,0,1:T(8,128)(2,1)} %copy.73), calls=%async_computation.2 | async-start | bytes 25165824 | tf_op jit(solution)/shard_map/all_to_all | solution.py:38
  50.4 0.0 copy-done.9
  50.4 0.1 copy.59
  50.5 0.1 eq.83
  50.7 0.1 eq.79
  50.9 18.1 %reduce-window.14 = s32[64,12,128]{2,1,0:T(8,128)S(1)} reduce-window(s32[64,12,128]{2,1,0:T(8,128)S(1)} %fusion.37, s32[]{:T(128)} %constant.52.clone.1), window={size=1x1x128 pad=0_0x0_0x127_0}, to_apply=%region_0.0 | reduce-window | flops 12484608 | bytes 786436 | tf_op jit(solution)/shard_map/reduce-window
  69.0 0.2 slice.112
  69.2 0.3 copy.61
  69.5 0.1 copy.62
  69.6 0.2 add_add_fusion.1
  69.8 0.1 fusion.42
  70.0 0.1 reduce_sum.47
  70.1 0.1 copy.63
  70.2 0.0 copy-start.7
  70.2 2.9 fusion.4
  73.2 5.0 convolution_convert_fusion.1
  78.1 5.6 copy.64
  83.7 0.0 copy-done.7
  83.7 105.1 %all-to-all-done.2 = bf16[8,8,48,2048]{3,2,0,1:T(8,128)(2,1)} async-done(((bf16[8,8,48,2048]{3,2,0,1:T(8,128)(2,1)}), bf16[8,8,48,2048]{3,2,0,1:T(8,128)(2,1)}, u32[]{:S(2)}, u32[]{:S(2)}) %all-to-all-start.2) | async-done | bytes 12582944 | tf_op jit(solution)/shard_map/all_to_all | solution.py:38
  188.8 6.7 %all-to-all-start = ((bf16[8,8,48,2048]{3,2,0,1:T(8,128)(2,1)}), bf16[8,8,48,2048]{3,2,0,1:T(8,128)(2,1)}, u32[]{:S(2)}, u32[]{:S(2)}) async-start(bf16[8,8,48,2048]{3,2,0,1:T(8,128)(2,1)} %copy.64), calls=%async_computation | async-start | bytes 25165824 | tf_op jit(solution)/shard_map/all_to_all | solution.py:38
  195.5 10.7 %copy.74 = bf16[8,8,48,2048]{3,2,1,0:T(8,128)(2,1)} copy(bf16[8,8,48,2048]{3,2,0,1:T(8,128)(2,1)} %all-to-all-done.2) | data formatting | bytes 25165824 | tf_op jit(solution)/shard_map/all_to_all | solution.py:38
  206.2 32.1 %fusion.62 = f32[8,384,1408]{2,1,0:T(8,128)} fusion(bf16[8,384,2048]{2,1,0:T(8,128)(2,1)} %bitcast.197, bf16[8,2048,1408]{2,1,0:T(8,128)(2,1)} %param.21), kind=kOutput, calls=%fused_computation.104 | convolution fusion | flops 17716740096 | bytes 76021760 | tf_op jit(solution)/shard_map/erd,edf->erf/dot_general | solution.py:20
  238.3 50.3 %convolution_convert_fusion.3 = bf16[8,384,2048]{2,1,0:T(8,128)(2,1)} fusion(bf16[8,1408,2048]{2,1,0:T(8,128)(2,1)} %param.23, f32[8,384,1408]{2,1,0:T(8,128)} %fusion.62, bf16[8,384,2048]{2,1,0:T(8,128)(2,1)} %bitcast.198, bf16[8,2048,1408]{2,1,0:T(8,128)(2,1)} %param.22), kind=kOutput, calls=%fused_computation.15 | convolution fusion | flops 35465723904 | bytes 134742016 | tf_op jit(solution)/shard_map/erf,efd->erd/dot_general | solution.py:23
  288.6 10.7 %copy.75 = bf16[8,8,48,2048]{3,2,0,1:T(8,128)(2,1)} copy(bf16[8,8,48,2048]{3,2,1,0:T(8,128)(2,1)} %bitcast.199) | data formatting | bytes 25165824 | tf_op jit(solution)/shard_map/reshape | solution.py:40
  299.3 34.6 %all-to-all-done = bf16[8,8,48,2048]{3,2,0,1:T(8,128)(2,1)} async-done(((bf16[8,8,48,2048]{3,2,0,1:T(8,128)(2,1)}), bf16[8,8,48,2048]{3,2,0,1:T(8,128)(2,1)}, u32[]{:S(2)}, u32[]{:S(2)}) %all-to-all-start) | async-done | bytes 12582944 | tf_op jit(solution)/shard_map/all_to_all | solution.py:38
  333.9 6.7 %all-to-all-start.3 = ((bf16[8,8,48,2048]{3,2,0,1:T(8,128)(2,1)}), bf16[8,8,48,2048]{3,2,0,1:T(8,128)(2,1)}, u32[]{:S(2)}, u32[]{:S(2)}) async-start(bf16[8,8,48,2048]{3,2,0,1:T(8,128)(2,1)} %copy.75), calls=%async_computation.3 | async-start | bytes 25165824 | tf_op jit(solution)/shard_map/all_to_all | solution.py:40
  340.6 10.7 %copy.65 = bf16[8,8,48,2048]{3,2,1,0:T(8,128)(2,1)} copy(bf16[8,8,48,2048]{3,2,0,1:T(8,128)(2,1)} %all-to-all-done) | data formatting | bytes 25165824 | tf_op jit(solution)/shard_map/all_to_all | solution.py:38
  351.3 32.1 %fusion.61 = f32[8,384,1408]{2,1,0:T(8,128)} fusion(bf16[8,384,2048]{2,1,0:T(8,128)(2,1)} %bitcast.200, bf16[8,2048,1408]{2,1,0:T(8,128)(2,1)} %param.21), kind=kOutput, calls=%fused_computation.103 | convolution fusion | flops 17716740096 | bytes 76021760 | tf_op jit(solution)/shard_map/erd,edf->erf/dot_general | solution.py:20
  383.4 50.3 %convolution_convert_fusion.4 = bf16[8,384,2048]{2,1,0:T(8,128)(2,1)} fusion(bf16[8,1408,2048]{2,1,0:T(8,128)(2,1)} %param.23, f32[8,384,1408]{2,1,0:T(8,128)} %fusion.61, bf16[8,384,2048]{2,1,0:T(8,128)(2,1)} %bitcast.201, bf16[8,2048,1408]{2,1,0:T(8,128)(2,1)} %param.22), kind=kOutput, calls=%fused_computation.16 | convolution fusion | flops 35465723904 | bytes 134742016 | tf_op jit(solution)/shard_map/erf,efd->erd/dot_general | solution.py:23
  433.7 10.7 %copy.66 = bf16[8,8,48,2048]{3,2,0,1:T(8,128)(2,1)} copy(bf16[8,8,48,2048]{3,2,1,0:T(8,128)(2,1)} %bitcast.202) | data formatting | bytes 25165824 | tf_op jit(solution)/shard_map/reshape | solution.py:40
  444.5 34.5 %all-to-all-done.3 = bf16[8,8,48,2048]{3,2,0,1:T(8,128)(2,1)} async-done(((bf16[8,8,48,2048]{3,2,0,1:T(8,128)(2,1)}), bf16[8,8,48,2048]{3,2,0,1:T(8,128)(2,1)}, u32[]{:S(2)}, u32[]{:S(2)}) %all-to-all-start.3) | async-done | bytes 12582944 | tf_op jit(solution)/shard_map/all_to_all | solution.py:40
  479.0 6.7 %all-to-all-start.1 = ((bf16[8,8,48,2048]{3,2,0,1:T(8,128)(2,1)}), bf16[8,8,48,2048]{3,2,0,1:T(8,128)(2,1)}, u32[]{:S(2)}, u32[]{:S(2)}) async-start(bf16[8,8,48,2048]{3,2,0,1:T(8,128)(2,1)} %copy.66), calls=%async_computation.1 | async-start | bytes 25165824 | tf_op jit(solution)/shard_map/all_to_all | solution.py:40
  485.7 0.0 copy-done.10
  485.8 12.7 %convolution_convert_fusion.2 = bf16[256,6144]{1,0:T(8,128)(2,1)} fusion(bf16[256,2048]{1,0:T(8,128)(2,1)S(1)} %copy-done.12, bf16[2048,6144]{1,0:T(8,128)(2,1)} %param.19), kind=kOutput, calls=%fused_computation.14 | convolution fusion | flops 6444023808 | bytes 29360128 | tf_op jit(solution)/shard_map/dot_general | solution.py:53
  498.5 6.5 copy.76
  505.0 22.7 %fusion = f32[256,6,2048]{2,0,1:T(8,128)} fusion(bf16[3072,2048,1]{1,0,2:T(8,128)(2,1)S(1)} %bitcast.203, s32[256,6]{0,1:T(8,128)S(1)} %copy-done.6), kind=kOutput, calls=%fused_computation.1 | convolution fusion | flops 19332071424 | bytes 25171968 | tf_op jit(solution)/shard_map/tjs,sd->tjd/dot_general | solution.py:41
  527.7 96.5 %all-to-all-done.1 = bf16[8,8,48,2048]{3,2,0,1:T(8,128)(2,1)} async-done(((bf16[8,8,48,2048]{3,2,0,1:T(8,128)(2,1)}), bf16[8,8,48,2048]{3,2,0,1:T(8,128)(2,1)}, u32[]{:S(2)}, u32[]{:S(2)}) %all-to-all-start.1) | async-done | bytes 12582944 | tf_op jit(solution)/shard_map/all_to_all | solution.py:40
  624.2 6.5 copy.67
  630.6 0.0 copy-start.4
  630.6 22.9 %fusion.2 = f32[256,6,2048]{2,0,1:T(8,128)} fusion(bf16[3072,2048,1]{1,0,2:T(8,128)(2,1)S(1)} %bitcast.204, s32[256,6]{0,1:T(8,128)S(1)} %copy-done.8), kind=kOutput, calls=%fused_computation.4 | convolution fusion | flops 19332071424 | bytes 25171968 | tf_op jit(solution)/shard_map/tjs,sd->tjd/dot_general | solution.py:41
  653.6 6.4 fusion.14
  659.9 2.3 copy-done.2
  662.2 0.2 copy-done.3
  662.4 2.0 fusion.27
  (22 shorter events, 0.2 us)
Async XLA Ops:
  0.6 24.3 %copy-start = (bf16[256,2048]{1,0:T(8,128)(2,1)S(1)}, bf16[256,2048]{1,0:T(8,128)(2,1)}, u32[]{:S(2)}) copy-start(bf16[256,2048]{1,0:T(8,128)(2,1)} %param.16) | copy-start | bytes 3145732
  21.9 2.9 copy-start.5
  42.3 8.1 %copy-start.9 = (s32[256,6]{0,1:T(8,128)S(1)}, s32[256,6]{0,1:T(8,128)}, u32[]{:S(2)}) copy-start(s32[256,6]{0,1:T(8,128)} %param.13) | copy-start | bytes 18436
  42.3 146.5 %all-to-all-start.2 = ((bf16[8,8,48,2048]{3,2,0,1:T(8,128)(2,1)}), bf16[8,8,48,2048]{3,2,0,1:T(8,128)(2,1)}, u32[]{:S(2)}, u32[]{:S(2)}) async-start(bf16[8,8,48,2048]{3,2,0,1:T(8,128)(2,1)} %copy.73), calls=%async_computation.2 | async-start | bytes 25165824 | tf_op jit(solution)/shard_map/all_to_all | solution.py:38
  70.2 13.5 %copy-start.7 = (s32[256,6]{0,1:T(8,128)}, s32[256,6]{0,1:T(8,128)S(1)}, u32[]{:S(2)}) copy-start(s32[256,6]{0,1:T(8,128)S(1)} %fusion.45) | copy-start | bytes 18436
  188.8 145.1 %all-to-all-start = ((bf16[8,8,48,2048]{3,2,0,1:T(8,128)(2,1)}), bf16[8,8,48,2048]{3,2,0,1:T(8,128)(2,1)}, u32[]{:S(2)}, u32[]{:S(2)}) async-start(bf16[8,8,48,2048]{3,2,0,1:T(8,128)(2,1)} %copy.64), calls=%async_computation | async-start | bytes 25165824 | tf_op jit(solution)/shard_map/all_to_all | solution.py:38
  333.9 145.1 %all-to-all-start.3 = ((bf16[8,8,48,2048]{3,2,0,1:T(8,128)(2,1)}), bf16[8,8,48,2048]{3,2,0,1:T(8,128)(2,1)}, u32[]{:S(2)}, u32[]{:S(2)}) async-start(bf16[8,8,48,2048]{3,2,0,1:T(8,128)(2,1)} %copy.75), calls=%async_computation.3 | async-start | bytes 25165824 | tf_op jit(solution)/shard_map/all_to_all | solution.py:40
  444.5 41.3 %copy-start.10 = (f32[256,6]{0,1:T(8,128)S(1)}, f32[256,6]{0,1:T(8,128)}, u32[]{:S(2)}) copy-start(f32[256,6]{0,1:T(8,128)} %param.18) | copy-start | bytes 18436
  444.5 41.3 %copy-start.11 = (f32[256,6]{0,1:T(8,128)S(1)}, f32[256,6]{0,1:T(8,128)}, u32[]{:S(2)}) copy-start(f32[256,6]{0,1:T(8,128)} %param.14) | copy-start | bytes 18436
  444.5 41.3 %copy-start.12 = (bf16[256,2048]{1,0:T(8,128)(2,1)S(1)}, bf16[256,2048]{1,0:T(8,128)(2,1)}, u32[]{:S(2)}) copy-start(bf16[256,2048]{1,0:T(8,128)(2,1)} %param.15) | copy-start | bytes 3145732
  479.0 145.2 %all-to-all-start.1 = ((bf16[8,8,48,2048]{3,2,0,1:T(8,128)(2,1)}), bf16[8,8,48,2048]{3,2,0,1:T(8,128)(2,1)}, u32[]{:S(2)}, u32[]{:S(2)}) async-start(bf16[8,8,48,2048]{3,2,0,1:T(8,128)(2,1)} %copy.66), calls=%async_computation.1 | async-start | bytes 25165824 | tf_op jit(solution)/shard_map/all_to_all | solution.py:40
  498.5 6.5 copy-start.6
  527.7 102.9 %copy-start.8 = (s32[256,6]{0,1:T(8,128)S(1)}, s32[256,6]{0,1:T(8,128)}, u32[]{:S(2)}) copy-start(s32[256,6]{0,1:T(8,128)} %copy-done.7) | copy-start | bytes 18436
  630.6 22.9 %copy-start.4 = (bf16[256,2048]{1,0:T(8,128)(2,1)S(1)}, bf16[256,2048]{1,0:T(8,128)(2,1)}, u32[]{:S(2)}) copy-start(bf16[256,2048]{1,0:T(8,128)(2,1)} %fusion.10) | copy-start | bytes 3145732
  653.6 8.6 %copy-start.2 = (f32[256,6,2048]{2,0,1:T(8,128)S(1)}, f32[256,6,2048]{2,0,1:T(8,128)}, u32[]{:S(2)}) copy-start(f32[256,6,2048]{2,0,1:T(8,128)} %fusion.2) | copy-start | bytes 37748740
  653.6 8.8 %copy-start.3 = (bf16[256,2048]{1,0:T(8,128)(2,1)S(1)}, bf16[256,2048]{1,0:T(8,128)(2,1)}, u32[]{:S(2)}) copy-start(bf16[256,2048]{1,0:T(8,128)(2,1)} %param.12) | copy-start | bytes 3145732
  653.6 10.8 %copy-start.1 = (bf16[256,2048]{1,0:T(8,128)(2,1)S(1)}, bf16[256,2048]{1,0:T(8,128)(2,1)}, u32[]{:S(2)}) copy-start(bf16[256,2048]{1,0:T(8,128)(2,1)} %param.16) | copy-start | bytes 3145732
where the time goes:
time: 672 us; the launch traced here: 665 us
  waiting for transfers between devices  271 us (40%)
  matrix products  240 us (36%)
  local copies, waits for them, and re-layouts  72.6 us (11%)
  other arithmetic  52.1 us (8%)
  starting transfers between devices  28.2 us (4%)
    all_to_all x2, waiting for transfers between devices, moe_local(): recv_buf = lax.all_to_all(send_buf, 'ep', 1, 1, tiled=True)  140 us
    all_to_all x2, waiting for transfers between devices, moe_local(): lax.all_to_all(expert_out.reshape(local_n, n_devs, capacity, model_dim),...  131 us
    dot_general x2, matrix products, expert_ffn(): jnp.einsum('erf,efd->erd', hidden, w_down, preferred_element_type=jnp.flo...  101 us
    dot_general x2, matrix products, expert_ffn(): jnp.einsum('erd,edf->erf', rows_in, w_gate, preferred_element_type=jnp.fl...  64.2 us
    dot_general x2, matrix products, moe_local(): jnp.einsum('tjs,sd->tjd', picker, back_buf.reshape(n_slots, model_dim), p...  45.6 us
    another operation x4, other arithmetic  36.3 us
    all_to_all x2, local copies, waits for them, and re-layouts, moe_local(): recv_buf = lax.all_to_all(send_buf, 'ep', 1, 1, tiled=True)  21.4 us
    reshape x2, local copies, waits for them, and re-layouts, moe_local(): expert_out.reshape(local_n, n_devs, capacity, model_dim)  21.4 us
  transfers between devices with their start and end apart: 4, of which 4 were waited for; matrix products, arithmetic and copies ran while one was open for 43% of the time, Pallas kernels for 0%

commit v1 on v0

v1 whole, which is shorter than its diff:
```python
import functools

import jax
import jax.numpy as jnp
from jax import lax
from jax.experimental import pallas as pl
from jax.experimental.pallas import tpu as pltpu
from jax.sharding import PartitionSpec as P

F32 = jnp.float32
BF16 = jnp.bfloat16
VMEM_LIMIT = 60 * 1024 * 1024


def routing_tables(route, gate, first_expert, local_n, capacity):
    n_src, _, tok_n = route.shape
    local = route - first_expert
    hits = local[:, :, None, :] == jnp.arange(local_n)[None, None, :, None]
    chosen = jnp.sum(hits.astype(F32), axis=1)
    gates = jnp.sum(jnp.where(hits, gate[:, :, None, :], 0.0), axis=1)
    before = (jnp.arange(tok_n)[:, None] < jnp.arange(tok_n)[None, :]).astype(BF16)
    rank = jnp.dot(chosen.reshape(n_src * local_n, tok_n).astype(BF16), before, preferred_element_type=F32)
    rank = rank.reshape(n_src, local_n, tok_n).astype(jnp.int32)
    rank = jnp.where(chosen > 0, rank, -1)
    slots = jnp.arange(capacity)
    place = (rank[:, :, None, :] == slots[None, None, :, None]).astype(BF16)
    place = place.reshape(n_src, local_n * capacity, tok_n)
    hi = lax.reduce_precision(gates, 8, 7)
    rest = gates - hi
    mid = lax.reduce_precision(rest, 8, 7)
    low = rest - mid
    parts = jnp.stack([hi, mid, low], axis=1)
    parts = jnp.swapaxes(parts, 2, 3)
    rank_t = jnp.swapaxes(rank, 1, 2)
    combine = jnp.where(
        rank_t[:, None, :, :, None] == slots[None, None, None, None, :], parts[:, :, :, :, None], 0.0
    ).astype(BF16)
    return place, combine.reshape(n_src, 3 * tok_n, local_n * capacity)


def dispatch(place, tokens, local_n, capacity):
    n_src, n_slots, tok_n = place.shape
    dim = tokens.shape[1]

    def body(place_ref, tok_ref, out_ref):
        rows = jnp.dot(place_ref[0], tok_ref[...], preferred_element_type=F32).astype(BF16)
        out_ref[:, 0] = rows.reshape(local_n, capacity, dim)

    return pl.pallas_call(
        body,
        grid=(n_src,),
        in_specs=[
            pl.BlockSpec((1, n_slots, tok_n), lambda s: (s, 0, 0)),
            pl.BlockSpec((tok_n, dim), lambda s: (s, 0)),
        ],
        out_specs=pl.BlockSpec((local_n, 1, capacity, dim), lambda s: (0, s, 0, 0)),
        out_shape=jax.ShapeDtypeStruct((local_n, n_src, capacity, dim), BF16),
        compiler_params=pltpu.CompilerParams(vmem_limit_bytes=VMEM_LIMIT),
        cost_estimate=pl.CostEstimate(
            flops=2 * n_src * n_slots * tok_n * dim, bytes_accessed=22_000_000, transcendentals=0
        ),
        name="dispatch",
    )(place, tokens)


def gate_up(rows, w_gate, w_up):
    local_n, row_n, dim = rows.shape
    ff = w_gate.shape[2]
    wide = 256
    n_full = ff // wide

    def body(rows_ref, wg_ref, wu_ref, out_ref):
        x = rows_ref[0]
        for i in range(n_full):
            cols = slice(i * wide, (i + 1) * wide)
            g = jnp.dot(x, wg_ref[0, :, cols], preferred_element_type=F32)
            u = jnp.dot(x, wu_ref[0, :, cols], preferred_element_type=F32)
            out_ref[0, :, cols] = (jax.nn.silu(g) * u).astype(BF16)
        if n_full * wide < ff:
            tail = ff - n_full * wide
            both = jnp.concatenate([wg_ref[0, :, n_full * wide :], wu_ref[0, :, n_full * wide :]], axis=1)
            gu = jnp.dot(x, both, preferred_element_type=F32)
            out_ref[0, :, n_full * wide :] = (jax.nn.silu(gu[:, :tail]) * gu[:, tail:]).astype(BF16)

    return pl.pallas_call(
        body,
        grid=(local_n,),
        in_specs=[
            pl.BlockSpec((1, row_n, dim), lambda e: (e, 0, 0)),
            pl.BlockSpec((1, dim, ff), lambda e: (e, 0, 0)),
            pl.BlockSpec((1, dim, ff), lambda e: (e, 0, 0)),
        ],
        out_specs=pl.BlockSpec((1, row_n, ff), lambda e: (e, 0, 0)),
        out_shape=jax.ShapeDtypeStruct((local_n, row_n, ff), BF16),
        compiler_params=pltpu.CompilerParams(vmem_limit_bytes=VMEM_LIMIT),
        cost_estimate=pl.CostEstimate(
            flops=4 * local_n * row_n * dim * ff,
            bytes_accessed=2 * local_n * (2 * dim * ff + row_n * (dim + ff)),
            transcendentals=local_n * row_n * ff,
        ),
        name="gate_up",
    )(rows, w_gate, w_up)


def down_mix(hidden, w_down, combine, chunk, n_chunks, capacity):
    local_n, row_n, ff = hidden.shape
    dim = w_down.shape[2]
    n_src, tok3, n_slots = combine.shape
    tok_n = tok3 // 3
    cols = dim // n_chunks

    def body(hid_ref, wd_ref, comb_ref, out_ref, y_ref):
        e = pl.program_id(0)
        y = jnp.dot(hid_ref[0], wd_ref[0], preferred_element_type=F32).astype(BF16)
        y_ref[:, e] = y.reshape(n_src, capacity, cols)

        @pl.when(e == local_n - 1)
        def _():
            for s in range(n_src):
                ys = y_ref[s].reshape(n_slots, cols)
                mix = jnp.dot(comb_ref[s], ys, preferred_element_type=F32)
                out_ref[s * tok_n : (s + 1) * tok_n] = (
                    mix[:tok_n] + mix[tok_n : 2 * tok_n] + mix[2 * tok_n :]
                )

    return pl.pallas_call(
        body,
        grid=(local_n,),
        in_specs=[
            pl.BlockSpec((1, row_n, ff), lambda e: (e, 0, 0)),
            pl.BlockSpec((1, ff, cols), lambda e: (e, 0, chunk)),
            pl.BlockSpec((n_src, tok3, n_slots), lambda e: (0, 0, 0)),
        ],
        out_specs=pl.BlockSpec((n_src * tok_n, cols), lambda e: (0, 0)),
        out_shape=jax.ShapeDtypeStruct((n_src * tok_n, cols), F32),
        scratch_shapes=[pltpu.VMEM((n_src, local_n, capacity, cols), BF16)],
        compiler_params=pltpu.CompilerParams(vmem_limit_bytes=VMEM_LIMIT),
        cost_estimate=pl.CostEstimate(
            flops=2 * local_n * row_n * ff * cols + 2 * n_src * tok3 * n_slots * cols,
            bytes_accessed=2 * local_n * (ff * cols + row_n * ff) + 4 * n_src * tok_n * cols,
            transcendentals=0,
        ),
        name="down_mix",
    )(hidden, w_down, combine)


def solution(mesh):
    n_devs = mesh.shape['ep']

    def local_step(x_a, route_a, gate_a, h_b, attn_b, route_b, gate_b, w_qkv, w_o, w_gate, w_up, w_down):
        tok_n, dim = x_a.shape
        top_k = route_a.shape[1]
        local_n = w_gate.shape[0]
        n_experts = local_n * n_devs
        capacity = min(tok_n, 2 * ((tok_n * top_k + n_experts - 1) // n_experts))
        me = lax.axis_index('ep')

        all_a = lax.all_gather(x_a, 'ep', axis=0, tiled=True)
        proj_b = jnp.dot(attn_b, w_o, preferred_element_type=F32).astype(BF16)
        mid_b = (h_b.astype(F32) + proj_b.astype(F32)).astype(BF16)
        all_b = lax.all_gather(mid_b, 'ep', axis=0, tiled=True)

        meta = jnp.concatenate([route_a.astype(F32).T, gate_a.T, route_b.astype(F32).T, gate_b.T], axis=0)
        meta = lax.all_gather(meta, 'ep', axis=0)
        k = top_k
        tables_a = routing_tables(meta[:, :k].astype(jnp.int32), meta[:, k : 2 * k], me * local_n, local_n, capacity)
        tables_b = routing_tables(
            meta[:, 2 * k : 3 * k].astype(jnp.int32), meta[:, 3 * k :], me * local_n, local_n, capacity
        )
        qkv_b = jnp.dot(h_b, w_qkv, preferred_element_type=F32).astype(BF16)

        def moe(tokens, all_tokens, tables):
            place, combine = tables
            n_chunks = 4
            rows = dispatch(place, all_tokens, local_n, capacity)
            hidden = gate_up(rows.reshape(local_n, n_devs * capacity, dim), w_gate, w_up)
            parts = []
            for chunk in range(n_chunks):
                part = down_mix(hidden, w_down, combine, chunk, n_chunks, capacity)
                parts.append(lax.psum_scatter(part, 'ep', scatter_dimension=0, tiled=True))
            mixture = jnp.concatenate(parts, axis=1)
            return (tokens.astype(F32) + mixture).astype(BF16)

        return moe(x_a, all_a, tables_a), moe(mid_b, all_b, tables_b), qkv_b

    row_spec = P(('dp', 'ep'), None)
    full_spec = P(None, None)
    expert_spec = P('ep', None, None)
    return jax.shard_map(
        local_step,
        mesh=mesh,
        in_specs=(row_spec, row_spec, row_spec, row_spec, row_spec, row_spec, row_spec, full_spec, full_spec, expert_spec, expert_spec, expert_spec),
        out_specs=(row_spec, row_spec, row_spec),
        check_vma=False,
    )
```

time: 672 us -> 447 us (0.67)
  Pallas kernels: 0 us -> 259 us
  matrix products: 240 us -> 20.1 us
  waiting for transfers between devices: 271 us -> 71.8 us
  local copies, waits for them, and re-layouts: 72.6 us -> 41.1 us
  other arithmetic: 52.1 us -> 20.9 us
  starting transfers between devices: 28.2 us -> 1.12 us
  blocking collectives: 0 us -> 15.2 us
  between operations: 1.44 us -> 14.4 us
    all_to_all x4 -> x0, waiting for transfers between devices: 271 us -> none  [the longest x2 140 us: moe_local(): recv_buf = lax.all_to_all(send_buf, 'ep', 1, 1, tiled=True)]
    pallas_call x0 -> x12, Pallas kernels: none -> 259 us  [the longest x8 144 us: down_mix(): pl.pallas_call(body, grid=(local_n,), in_specs=[pl.BlockSpec((1, row_n, f...]
    dot_general x10 -> x4, matrix products: 240 us -> 20.1 us  [the longest x1 12.9 us: local_step(): qkv_b = jnp.dot(h_b, w_qkv, preferred_element_type=F32).astype(BF16)]
    reduce_scatter x0 -> x8, waiting for transfers between devices: none -> 69.3 us  [moe(): parts.append(lax.psum_scatter(part, 'ep', scatter_dimension=0, tiled=True))]
    convert_element_type x0 -> x4, local copies, waits for them, and re-layouts: none -> 39.3 us  [routing_tables(): combine = jnp.where(rank_t[:, None, :, :, None] == slots[None, None, None...]
    another operation x4 -> x0, other arithmetic: 36.3 us -> none
    all_to_all x4 -> x0, local copies, waits for them, and re-layouts: 34.4 us -> none  [the longest x2 21.4 us: moe_local(): recv_buf = lax.all_to_all(send_buf, 'ep', 1, 1, tiled=True)]
    reshape x4 -> x0, local copies, waits for them, and re-layouts: 32.5 us -> none  [the longest x2 21.4 us: moe_local(): expert_out.reshape(local_n, n_devs, capacity, model_dim)]
  transfers between devices with their start and end apart: 4 -> 10, of which waited for: 4 -> 3; matrix products, arithmetic and copies ran while one was open for 43% -> 18% of each run, Pallas kernels for 0% -> 58%
where the time goes in v1:
time: 447 us; the launch traced here: 443 us
  Pallas kernels  259 us (58%)
  waiting for transfers between devices  71.8 us (16%)
  local copies, waits for them, and re-layouts  41.1 us (9%)
  other arithmetic  20.9 us (5%)
  matrix products  20.1 us (4%)
  blocking collectives  15.2 us (3%)
  between operations  14.4 us (3%)
    pallas_call x8, Pallas kernels, down_mix(): pl.pallas_call(body, grid=(local_n,), in_specs=[pl.BlockSpec((1, row_n, f...  144 us
    pallas_call x2, Pallas kernels, gate_up(): pl.pallas_call(body, grid=(local_n,), in_specs=[pl.BlockSpec((1, row_n, d...  89.3 us
    reduce_scatter x8, waiting for transfers between devices, moe(): parts.append(lax.psum_scatter(part, 'ep', scatter_dimension=0, tiled=True))  69.3 us
    convert_element_type x4, local copies, waits for them, and re-layouts, routing_tables(): combine = jnp.where(rank_t[:, None, :, :, None] == slots[None, None, None...  39.3 us
    pallas_call x2, Pallas kernels, dispatch(): pl.pallas_call(body, grid=(n_src,), in_specs=[pl.BlockSpec((1, n_slots, t...  25 us
    all_gather x1, blocking collectives, local_step(): meta = lax.all_gather(meta, 'ep', axis=0)  15.2 us
    dot_general x1, matrix products, local_step(): qkv_b = jnp.dot(h_b, w_qkv, preferred_element_type=F32).astype(BF16)  12.9 us
    convert_element_type x2, other arithmetic, routing_tables(): combine = jnp.where(rank_t[:, None, :, :, None] == slots[None, None, None...  11.6 us
  transfers between devices with their start and end apart: 10, of which 3 were waited for; matrix products, arithmetic and copies ran while one was open for 18% of the time, Pallas kernels for 58%

profile of v1, /device:TPU:81, one launch (start us, length us, event | category | flops | bytes accessed | tf_op | source)
XLA Modules:
  0.0 443.4 jit_solution(17806086498711450405)
XLA Ops:
  7.2 0.0 copy-start
  7.2 0.1 all-gather.4.cloned.1.call-start
  7.3 0.7 all-gather.4.cloned.1.call-update
  8.0 0.0 copy-start.5
  8.0 0.1 all-gather.6.cloned.1.call-start
  8.1 0.3 copy-done
  8.4 6.9 %fusion.4 = bf16[256,2048]{1,0:T(8,128)(2,1)} fusion(bf16[256,2048]{1,0:T(8,128)(2,1)S(1)} %copy-done, bf16[2048,2048]{1,0:T(8,128)(2,1)} %param.20, bf16[256,2048]{1,0:T(8,128)(2,1)} %param.15), kind=kOutput, calls=%fused_computation.12 | convolution fusion | flops 2150105088 | bytes 11534336 | tf_op jit(solution)/shard_map/dot_general | solution.py:159
  15.3 0.1 all-gather.6.cloned.1.call-update
  15.4 0.1 reduce-scatter.15.cloned.1.call-start
  15.5 0.1 eq.108
  15.6 15.2 %all-gather = f32[192,256]{1,0:T(8,128)S(1)} all-gather(f32[24,256]{1,0:T(8,128)S(1)} %pad_maximum_fusion), channel_id=2, replica_groups=mesh['dp'=4,'ep'=8] {'ep'}, dimensions={0}, use_global_device_ids=true | all-gather | bytes 221184 | tf_op jit(solution)/shard_map/all_gather | solution.py:164
  30.9 0.1 select_reduce_fusion.1
  31.0 0.1 copy.25
  31.1 0.2 fusion.8
  31.3 0.5 iota_compare_fusion.1
  31.8 5.8 %select_convert_fusion.1 = bf16[8,3,256,8,48]{2,1,4,3,0:T(4,128)(2,1)} fusion(bf16[8,3,256,8]{2,1,3,0:T(4,128)(2,1)S(1)} %copy.25, pred[8,256,8,48]{1,3,2,0:T(8,128)(4,1)S(1)} %iota_compare_fusion.1), kind=kLoop, calls=%fused_computation.1 | loop fusion | flops 2359296 | bytes 5603328 | tf_op jit(solution)/shard_map/convert_element_type | solution.py:37
  37.6 13.0 %convert_element_type.96 = bf16[8,768,384]{1,2,0:T(8,128)(2,1)} reshape(bf16[8,3,256,8,48]{2,1,4,3,0:T(4,128)(2,1)} %select_convert_fusion.1) | data formatting | bytes 9437184 | tf_op jit(solution)/shard_map/convert_element_type | solution.py:37
  50.6 6.6 %copy.26.comb_ref = bf16[8,768,384]{2,1,0:T(8,128)(2,1)} copy(bf16[8,768,384]{1,2,0:T(8,128)(2,1)} %convert_element_type.96) | data formatting | bytes 9437184 | tf_op jit(solution)/shard_map/convert_element_type | solution.py:37
  57.2 0.1 select_reduce_fusion
  57.3 0.2 fusion.7
  57.5 2.4 fusion.1
  59.9 1.3 all-gather.4.cloned.1.call-done.tok_ref
  61.2 12.5 %dispatch.2 = bf16[8,8,48,2048]{3,2,1,0:T(8,128)(2,1)} custom-call(bf16[8,384,256]{2,1,0:T(8,128)(2,1)} %get-tuple-element.18.place_ref, bf16[2048,2048]{1,0:T(8,128)(2,1)} %all-gather.4.cloned.1.call-done.tok_ref), custom_call_target="tpu_custom_call" | custom-call | flops 3221225472 | bytes 22000000 | tf_op jit(solution)/shard_map/dispatch/pallas_call | solution.py:49
  73.7 44.7 %gate_up.2.hid_ref = bf16[8,384,1408]{2,1,0:T(8,128)(2,1)} custom-call(bf16[8,384,2048]{2,1,0:T(8,128)(2,1)} %bitcast.61, bf16[8,2048,1408]{2,1,0:T(8,128)(2,1)} %wg_ref.3, bf16[8,2048,1408]{2,1,0:T(8,128)(2,1)} %wu_ref.3), custom_call_target="tpu_custom_call" | custom-call | flops 35433480192 | bytes 113508352 | tf_op jit(solution)/shard_map/gate_up/pallas_call | solution.py:85
  118.4 18.1 %down_mix.11 = f32[2048,512]{1,0:T(8,128)} custom-call(bf16[8,384,1408]{2,1,0:T(8,128)(2,1)} %gate_up.2.hid_ref, bf16[8,1408,2048]{2,1,0:T(8,128)(2,1)} %wd_ref.15, bf16[8,768,384]{2,1,0:T(8,128)(2,1)} %copy.26.comb_ref), custom_call_target="tpu_custom_call" | custom-call | flops 6845104128 | bytes 24379392 | tf_op jit(solution)/shard_map/down_mix/pallas_call | solution.py:126
  136.5 0.1 reduce-scatter.15.cloned.1.call-update
  136.5 0.1 reduce-scatter.13.cloned.1.call-start
  136.6 18.0 %down_mix.10 = f32[2048,512]{1,0:T(8,128)} custom-call(bf16[8,384,1408]{2,1,0:T(8,128)(2,1)} %gate_up.2.hid_ref, bf16[8,1408,2048]{2,1,0:T(8,128)(2,1)} %wd_ref.15, bf16[8,768,384]{2,1,0:T(8,128)(2,1)} %copy.26.comb_ref), custom_call_target="tpu_custom_call" | custom-call | flops 6845104128 | bytes 24379392 | tf_op jit(solution)/shard_map/down_mix/pallas_call | solution.py:126
  154.7 0.1 reduce-scatter.13.cloned.1.call-update
  154.7 0.3 reduce-scatter.11.cloned.1.call-start
  155.0 18.1 %down_mix.9 = f32[2048,512]{1,0:T(8,128)} custom-call(bf16[8,384,1408]{2,1,0:T(8,128)(2,1)} %gate_up.2.hid_ref, bf16[8,1408,2048]{2,1,0:T(8,128)(2,1)} %wd_ref.15, bf16[8,768,384]{2,1,0:T(8,128)(2,1)} %copy.26.comb_ref), custom_call_target="tpu_custom_call" | custom-call | flops 6845104128 | bytes 24379392 | tf_op jit(solution)/shard_map/down_mix/pallas_call | solution.py:126
  173.1 0.1 reduce-scatter.11.cloned.1.call-update
  173.2 0.1 reduce-scatter.9.cloned.1.call-start
  173.2 18.0 %down_mix.8 = f32[2048,512]{1,0:T(8,128)} custom-call(bf16[8,384,1408]{2,1,0:T(8,128)(2,1)} %gate_up.2.hid_ref, bf16[8,1408,2048]{2,1,0:T(8,128)(2,1)} %wd_ref.15, bf16[8,768,384]{2,1,0:T(8,128)(2,1)} %copy.26.comb_ref), custom_call_target="tpu_custom_call" | custom-call | flops 6845104128 | bytes 24379392 | tf_op jit(solution)/shard_map/down_mix/pallas_call | solution.py:126
  191.2 0.1 reduce-scatter.9.cloned.1.call-update
  191.3 0.1 reduce-scatter.23.cloned.1.call-start
  191.4 0.1 copy.30
  191.5 0.5 iota_compare_fusion
  192.0 5.8 %select_convert_fusion = bf16[8,3,256,8,48]{2,1,4,3,0:T(4,128)(2,1)} fusion(bf16[8,3,256,8]{2,1,3,0:T(4,128)(2,1)S(1)} %copy.30, pred[8,256,8,48]{1,3,2,0:T(8,128)(4,1)S(1)} %iota_compare_fusion), kind=kLoop, calls=%fused_computation | loop fusion | flops 2359296 | bytes 5603328 | tf_op jit(solution)/shard_map/convert_element_type | solution.py:37
  197.8 13.0 %convert_element_type.109 = bf16[8,768,384]{1,2,0:T(8,128)(2,1)} reshape(bf16[8,3,256,8,48]{2,1,4,3,0:T(4,128)(2,1)} %select_convert_fusion) | data formatting | bytes 9437184 | tf_op jit(solution)/shard_map/convert_element_type | solution.py:37
  210.8 6.6 %copy.31.comb_ref = bf16[8,768,384]{2,1,0:T(8,128)(2,1)} copy(bf16[8,768,384]{1,2,0:T(8,128)(2,1)} %convert_element_type.109) | data formatting | bytes 9437184 | tf_op jit(solution)/shard_map/convert_element_type | solution.py:37
  217.5 12.5 %dispatch.3 = bf16[8,8,48,2048]{3,2,1,0:T(8,128)(2,1)} custom-call(bf16[8,384,256]{2,1,0:T(8,128)(2,1)} %get-tuple-element.17.place_ref, bf16[2048,2048]{1,0:T(8,128)(2,1)} %all-gather.6.cloned.1.call-done.tok_ref), custom_call_target="tpu_custom_call" | custom-call | flops 3221225472 | bytes 22000000 | tf_op jit(solution)/shard_map/dispatch/pallas_call | solution.py:49
  230.0 44.7 %gate_up.3.hid_ref = bf16[8,384,1408]{2,1,0:T(8,128)(2,1)} custom-call(bf16[8,384,2048]{2,1,0:T(8,128)(2,1)} %bitcast.62, bf16[8,2048,1408]{2,1,0:T(8,128)(2,1)} %wg_ref.3, bf16[8,2048,1408]{2,1,0:T(8,128)(2,1)} %wu_ref.3), custom_call_target="tpu_custom_call" | custom-call | flops 35433480192 | bytes 113508352 | tf_op jit(solution)/shard_map/gate_up/pallas_call | solution.py:85
  274.6 18.1 %down_mix.15 = f32[2048,512]{1,0:T(8,128)} custom-call(bf16[8,384,1408]{2,1,0:T(8,128)(2,1)} %gate_up.3.hid_ref, bf16[8,1408,2048]{2,1,0:T(8,128)(2,1)} %wd_ref.15, bf16[8,768,384]{2,1,0:T(8,128)(2,1)} %copy.31.comb_ref), custom_call_target="tpu_custom_call" | custom-call | flops 6845104128 | bytes 24379392 | tf_op jit(solution)/shard_map/down_mix/pallas_call | solution.py:126
  292.7 0.1 reduce-scatter.23.cloned.1.call-update
  292.8 0.3 reduce-scatter.21.cloned.1.call-start
  293.1 18.0 %down_mix.14 = f32[2048,512]{1,0:T(8,128)} custom-call(bf16[8,384,1408]{2,1,0:T(8,128)(2,1)} %gate_up.3.hid_ref, bf16[8,1408,2048]{2,1,0:T(8,128)(2,1)} %wd_ref.15, bf16[8,768,384]{2,1,0:T(8,128)(2,1)} %copy.31.comb_ref), custom_call_target="tpu_custom_call" | custom-call | flops 6845104128 | bytes 24379392 | tf_op jit(solution)/shard_map/down_mix/pallas_call | solution.py:126
  311.1 0.1 reduce-scatter.21.cloned.1.call-update
  311.2 0.1 reduce-scatter.19.cloned.1.call-start
  311.3 18.0 %down_mix.13 = f32[2048,512]{1,0:T(8,128)} custom-call(bf16[8,384,1408]{2,1,0:T(8,128)(2,1)} %gate_up.3.hid_ref, bf16[8,1408,2048]{2,1,0:T(8,128)(2,1)} %wd_ref.15, bf16[8,768,384]{2,1,0:T(8,128)(2,1)} %copy.31.comb_ref), custom_call_target="tpu_custom_call" | custom-call | flops 6845104128 | bytes 24379392 | tf_op jit(solution)/shard_map/down_mix/pallas_call | solution.py:126
  329.3 0.1 reduce-scatter.19.cloned.1.call-update
  329.3 0.1 reduce-scatter.17.cloned.1.call-start
  329.4 18.0 %down_mix.12 = f32[2048,512]{1,0:T(8,128)} custom-call(bf16[8,384,1408]{2,1,0:T(8,128)(2,1)} %gate_up.3.hid_ref, bf16[8,1408,2048]{2,1,0:T(8,128)(2,1)} %wd_ref.15, bf16[8,768,384]{2,1,0:T(8,128)(2,1)} %copy.31.comb_ref), custom_call_target="tpu_custom_call" | custom-call | flops 6845104128 | bytes 24379392 | tf_op jit(solution)/shard_map/down_mix/pallas_call | solution.py:126
  347.4 0.1 reduce-scatter.17.cloned.1.call-update
  347.5 1.2 copy-done.8
  348.7 12.9 %convolution_convert_fusion = bf16[256,6144]{1,0:T(8,128)(2,1)} fusion(bf16[256,2048]{1,0:T(8,128)(2,1)S(1)} %copy-done.8, bf16[2048,6144]{1,0:T(8,128)(2,1)} %param.19), kind=kOutput, calls=%fused_computation.2 | convolution fusion | flops 6444023808 | bytes 29360128 | tf_op jit(solution)/shard_map/dot_general | solution.py:170
  361.5 0.0 reduce-scatter.11.cloned.1.call-done
  361.6 0.0 reduce-scatter.9.cloned.1.call-done
  361.6 0.0 copy-done.2
  361.6 2.8 fusion.5
  364.5 33.4 %reduce-scatter.19.cloned.1.call-done = f32[256,512]{1,0:T(8,128)} async-done(((f32[2048,512]{1,0:T(8,128)}), f32[256,512]{1,0:T(8,128)}) %reduce-scatter.19.cloned.1.call-update) | async-done | bytes 524304 | tf_op jit(solution)/shard_map/reduce_scatter | solution.py:180
  397.9 35.9 %reduce-scatter.17.cloned.1.call-done = f32[256,512]{1,0:T(8,128)} async-done(((f32[2048,512]{1,0:T(8,128)}), f32[256,512]{1,0:T(8,128)}) %reduce-scatter.17.cloned.1.call-update) | async-done | bytes 524304 | tf_op jit(solution)/shard_map/reduce_scatter | solution.py:180
  433.8 0.0 copy-done.3
  433.8 2.8 fusion.6
  (26 shorter events, 0.2 us)
Async XLA Ops:
  7.2 1.2 copy-start
  7.2 54.0 %all-gather.4.cloned.1.call-start = ((), (), s32[]{:S(2)}) async-start(), calls=%async_computation.8 | async-start | bytes 9437184 | tf_op jit(solution)/shard_map/all_gather | solution.py:158
  8.0 7.6 %copy-start.6 = (s32[256,6]{0,1:T(8,128)S(1)}, s32[256,6]{0,1:T(8,128)}, u32[]{:S(2)}) copy-start(s32[256,6]{0,1:T(8,128)} %param.17) | copy-start | bytes 18436
  8.0 7.6 %copy-start.7 = (s32[256,6]{0,1:T(8,128)S(1)}, s32[256,6]{0,1:T(8,128)}, u32[]{:S(2)}) copy-start(s32[256,6]{0,1:T(8,128)} %param.13) | copy-start | bytes 18436
  8.0 7.6 %copy-start.4 = (f32[256,6]{0,1:T(8,128)S(1)}, f32[256,6]{0,1:T(8,128)}, u32[]{:S(2)}) copy-start(f32[256,6]{0,1:T(8,128)} %param.18) | copy-start | bytes 18436
  8.0 7.6 %copy-start.5 = (f32[256,6]{0,1:T(8,128)S(1)}, f32[256,6]{0,1:T(8,128)}, u32[]{:S(2)}) copy-start(f32[256,6]{0,1:T(8,128)} %param.14) | copy-start | bytes 18436
  8.0 209.4 %all-gather.6.cloned.1.call-start = ((), (), s32[]{:S(2)}) async-start(), calls=%async_computation.13 | async-start | bytes 9437184 | tf_op jit(solution)/shard_map/all_gather | solution.py:161
  15.4 346.2 %reduce-scatter.15.cloned.1.call-start = ((), (), s32[]{:S(2)}) async-start(), calls=%async_computation.12 | async-start | bytes 4718592 | tf_op jit(solution)/shard_map/reduce_scatter | solution.py:180
  136.5 225.0 %reduce-scatter.13.cloned.1.call-start = ((), (), s32[]{:S(2)}) async-start(), calls=%async_computation.11 | async-start | bytes 4718592 | tf_op jit(solution)/shard_map/reduce_scatter | solution.py:180
  154.7 206.8 %reduce-scatter.11.cloned.1.call-start = ((), (), s32[]{:S(2)}) async-start(), calls=%async_computation.10 | async-start | bytes 4718592 | tf_op jit(solution)/shard_map/reduce_scatter | solution.py:180
  173.2 188.4 %reduce-scatter.9.cloned.1.call-start = ((), (), s32[]{:S(2)}) async-start(), calls=%async_computation.9 | async-start | bytes 4718592 | tf_op jit(solution)/shard_map/reduce_scatter | solution.py:180
  191.3 173.2 %reduce-scatter.23.cloned.1.call-start = ((), (), s32[]{:S(2)}) async-start(), calls=%async_computation.17 | async-start | bytes 4718592 | tf_op jit(solution)/shard_map/reduce_scatter | solution.py:180
  292.8 71.7 %reduce-scatter.21.cloned.1.call-start = ((), (), s32[]{:S(2)}) async-start(), calls=%async_computation.16 | async-start | bytes 4718592 | tf_op jit(solution)/shard_map/reduce_scatter | solution.py:180
  311.2 86.7 %reduce-scatter.19.cloned.1.call-start = ((), (), s32[]{:S(2)}) async-start(), calls=%async_computation.15 | async-start | bytes 4718592 | tf_op jit(solution)/shard_map/reduce_scatter | solution.py:180
  329.3 104.4 %reduce-scatter.17.cloned.1.call-start = ((), (), s32[]{:S(2)}) async-start(), calls=%async_computation.14 | async-start | bytes 4718592 | tf_op jit(solution)/shard_map/reduce_scatter | solution.py:180
  347.4 1.2 copy-start.8
  348.7 12.9 %copy-start.2 = (bf16[256,2048]{1,0:T(8,128)(2,1)S(1)}, bf16[256,2048]{1,0:T(8,128)(2,1)}, u32[]{:S(2)}) copy-start(bf16[256,2048]{1,0:T(8,128)(2,1)} %param.12) | copy-start | bytes 3145732
  348.7 87.9 %copy-start.1 = (bf16[256,2048]{1,0:T(8,128)(2,1)S(1)}, bf16[256,2048]{1,0:T(8,128)(2,1)}, u32[]{:S(2)}) copy-start(bf16[256,2048]{1,0:T(8,128)(2,1)} %param.16) | copy-start | bytes 3145732
  361.5 72.2 %copy-start.3 = (bf16[256,2048]{1,0:T(8,128)(2,1)S(1)}, bf16[256,2048]{1,0:T(8,128)(2,1)}, u32[]{:S(2)}) copy-start(bf16[256,2048]{1,0:T(8,128)(2,1)} %fusion.4) | copy-start | bytes 3145732
Sparse Core Ops, SparseCore 0:
  9.7 51.4 all-gather.3
  63.4 46.6 all-gather.5
  136.7 32.8 reduce-scatter.14
  171.8 33.7 reduce-scatter.12
  207.7 33.7 reduce-scatter.10
  243.6 33.5 reduce-scatter.8
  292.9 32.8 reduce-scatter.22
  328.1 33.7 reduce-scatter.20
  364.2 33.6 reduce-scatter.18
  400.1 33.6 reduce-scatter.16

commit v2 on v0

v2 whole, which is shorter than its diff:
```python
import jax
import jax.numpy as jnp
from jax import lax
from jax.experimental import pallas as pl
from jax.experimental.pallas import tpu as pltpu
from jax.sharding import PartitionSpec as P

F32 = jnp.float32
BF16 = jnp.bfloat16
VMEM_LIMIT = 67_000_000
WIDE = 256
SLOTS = 4
CHUNKS = 4


def rem(a, b):
    return lax.rem(a, jnp.int32(b))


def div(a, b):
    return lax.div(a, jnp.int32(b))


def moe_kernel(
    capacity,
    x_a, h_b, attn_b, meta, w_qkv, w_o, w_gate, w_up, w_down,
    out_a, out_b, qkv, land,
    wbuf, rows, hidden, src_rows, expert_out, mixer, partial, pair, transit, near, out_stage, own_stage, table,
    w_sem, gather_send, gather_recv, meta_send, meta_recv, load_sem, stage_sem, own_sem,
    pair_send, pair_recv, far_send, far_recv, near_send, near_recv, credit,
):
    n_devs = land.shape[1]
    n_chips = n_devs // 2
    tok_n, dim = x_a.shape
    half_n = tok_n // 2
    local_n, row_n, ff = hidden.shape
    n_slots = local_n * capacity
    cols = dim // CHUNKS
    half = cols // 2
    n_full, tail = ff // WIDE, ff % WIDE
    gu_tiles = n_full + 1

    me = lax.axis_index('ep')
    chip, core = div(me, 2), rem(me, 2)
    partner = me + 1 - 2 * core
    right, left = rem(me + 2, n_devs), rem(me + n_devs - 2, n_devs)
    sides = (right, left)
    chip_right, chip_left, chip_far = rem(chip + 1, n_chips), rem(chip + n_chips - 1, n_chips), rem(chip + 2, n_chips)
    chip_side = (chip_right, chip_left)
    far = 2 * chip_far + core

    def remote(src, dst, send, recv, dev):
        return pltpu.make_async_remote_copy(
            src_ref=src, dst_ref=dst, send_sem=send, recv_sem=recv, device_id={'ep': dev},
            device_id_type=pl.DeviceIdType.MESH,
        )

    def sl(start, size):
        return pl.ds(pl.multiple_of(start, size), size)

    def tile_copies(phase, i):
        slot = rem(i, SLOTS)
        if phase in ('proj', 'qkv'):
            w = w_o if phase == 'proj' else w_qkv
            return ((None, [(w.at[:, sl(i * cols, cols)], wbuf.at[slot, :, 0:cols], w_sem.at[slot, 0])]),)
        if phase == 'down':
            n, e = div(i, local_n), rem(i, local_n)
            return ((None, [(w_down.at[e, :, sl(n * cols, cols)], wbuf.at[slot, 0:ff, 0:cols], w_sem.at[slot, 0])]),)
        e, t = div(i, gu_tiles), rem(i, gu_tiles)
        full = [
            (w_gate.at[e, :, sl(t * WIDE, WIDE)], wbuf.at[slot, :, 0:WIDE], w_sem.at[slot, 0]),
            (w_up.at[e, :, sl(t * WIDE, WIDE)], wbuf.at[slot, :, WIDE : 2 * WIDE], w_sem.at[slot, 1]),
        ]
        part = [
            (w_gate.at[e, :, n_full * WIDE : ff], wbuf.at[slot, :, 0:tail], w_sem.at[slot, 0]),
            (w_up.at[e, :, n_full * WIDE : ff], wbuf.at[slot, :, tail : 2 * tail], w_sem.at[slot, 1]),
        ]
        return ((t < n_full, full), (t == n_full, part))

    def fetch(phase, i):
        for cond, copies in tile_copies(phase, i):
            def go(copies=copies):
                for c in copies:
                    pltpu.make_async_copy(*c).start()
            if cond is None:
                go()
            else:
                pl.when(cond)(go)

    def arrive(phase, i, which=0):
        for c in tile_copies(phase, i)[which][1]:
            pltpu.make_async_copy(*c).wait()

    count = {'proj': CHUNKS, 'qkv': qkv.shape[1] // cols, 'gate_up': local_n * gu_tiles, 'down': CHUNKS * local_n}
    ahead = SLOTS - 1

    def next_tile(phase, following, i):
        @pl.when(i + ahead < count[phase])
        def _():
            fetch(phase, i + ahead)

        if following is not None:
            @pl.when(i + ahead >= count[phase])
            def _():
                fetch(following, i + ahead - count[phase])

    def own(m):
        return x_a if m == 0 else land.at[m, me]

    def rows_half(ref, hf):
        return ref.at[hf * half_n : (hf + 1) * half_n]

    def g_partner(m):
        return remote(own(m), land.at[m, me], gather_send.at[m, 0], gather_recv.at[m, 0], partner)

    def g_near(m, d, hf):
        k = 1 + 2 * d + hf
        return remote(
            rows_half(own(m), hf), rows_half(land.at[m, me], hf), gather_send.at[m, k], gather_recv.at[m, k], sides[d]
        )

    def g_forward(m, d):
        block = rows_half(land.at[m, sides[1 - d]], d)
        return remote(block, block, gather_send.at[m, 5 + d], gather_recv.at[m, 5 + d], sides[d])

    def g_pass(m, d):
        block = land.at[m, sides[1 - d]]
        return remote(block, block, gather_send.at[m, 7 + d], gather_recv.at[m, 7 + d], partner)

    def g_pass_far(m, d):
        block = rows_half(land.at[m, far], d)
        return remote(block, block, gather_send.at[m, 9 + d], gather_recv.at[m, 9 + d], partner)

    def gather_start(m):
        g_partner(m).start()
        for step in range(2):
            for d in range(2):
                g_near(m, d, d if step == 0 else 1 - d).start()

    def gather_forward(m):
        for d in range(2):
            g_near(m, d, d).wait_recv()
            g_forward(m, d).start()

    def gather_pass(m):
        for d in range(2):
            g_near(m, d, 1 - d).wait_recv()
            g_pass(m, d).start()

    def gather_near_done(m):
        g_partner(m).wait_recv()
        for d in range(2):
            g_pass(m, d).wait_recv()

    def gather_pass_far(m):
        for d in range(2):
            g_forward(m, d).wait_recv()
            g_pass_far(m, d).start()

    def gather_done(m):
        for d in range(2):
            g_pass_far(m, d).wait_recv()
        g_partner(m).wait_send()
        for d in range(2):
            g_near(m, d, 0).wait_send()
            g_near(m, d, 1).wait_send()
            g_forward(m, d).wait_send()
            g_pass(m, d).wait_send()
            g_pass_far(m, d).wait_send()

    def source_at(k):
        kk = div(k, 2)
        off = kk + div(kk, 2) - 2 * div(kk, 3)
        return 2 * rem(chip + off, n_chips) + rem(k, 2)

    def load(m, k):
        return pltpu.make_async_copy(land.at[m, source_at(k)], src_rows.at[rem(k, 2)], load_sem.at[rem(k, 2)])

    def dispatch(m, lo, hi):
        load(m, jnp.int32(lo)).start()

        def body(k, carry):
            @pl.when(k + 1 < hi)
            def _():
                load(m, k + 1).start()

            s, slot = source_at(k), rem(k, 2)
            load(m, k).wait()
            rank = table[s, m, 0:local_n]
            slots = lax.broadcasted_iota(jnp.int32, (capacity, tok_n), 0).astype(F32)
            pick = jnp.concatenate(
                [jnp.where(rank[e : e + 1] == slots, 1.0, 0.0).astype(BF16) for e in range(local_n)], axis=0
            )
            for j in range(CHUNKS):
                part = slice(j * cols, (j + 1) * cols)
                got = jnp.dot(pick, src_rows[slot, :, part], preferred_element_type=F32).astype(BF16)
                for e in range(local_n):
                    rows[e, pl.ds(pl.multiple_of(s * capacity, capacity), capacity), part] = got[
                        e * capacity : (e + 1) * capacity
                    ]
            return carry

        lax.fori_loop(jnp.int32(lo), jnp.int32(hi), body, 0)

    def make_mixer(m):
        lane = lax.broadcasted_iota(jnp.int32, (2 * local_n, n_slots), 1)
        line = lax.broadcasted_iota(jnp.int32, (2 * local_n, n_slots), 0)

        def spread(first):
            low = (line - first) * capacity
            inside = (line >= first) & (line < first + local_n) & (lane >= low) & (lane < low + capacity)
            return jnp.where(inside, 1.0, 0.0).astype(BF16)

        spread_rank, spread_gate = spread(0), spread(local_n)
        at = lax.broadcasted_iota(jnp.int32, (tok_n, n_slots), 1)
        base = jnp.zeros_like(at)
        for e in range(1, local_n):
            base = base + jnp.where(at >= e * capacity, capacity, 0)
        at = (at - base).astype(F32)

        def body(s, carry):
            value = table[s, m]
            hi = value.astype(BF16)
            rest = value - hi.astype(F32)
            mid = rest.astype(BF16)
            low = (rest - mid.astype(F32)).astype(BF16)

            def turn(v, e):
                return lax.dot_general(v, e, (((0,), (0,)), ((), ())), preferred_element_type=F32)

            here = turn(hi, spread_rank) == at
            for k, v in enumerate((hi, mid, low)):
                mixer[s, k * tok_n : (k + 1) * tok_n] = jnp.where(here, turn(v, spread_gate), 0.0).astype(BF16)
            return carry

        lax.fori_loop(jnp.int32(0), jnp.int32(n_devs), body, 0)

    def r_pair(n):
        return remote(partial.at[1 - core], pair.at[n], pair_send.at[n], pair_recv.at[n], partner)

    def r_far(n, d):
        return remote(pair.at[n, chip_far, d], transit.at[n, d], far_send.at[n, d], far_recv.at[n, d], sides[d])

    def r_near(n, d, hf):
        return remote(
            pair.at[n, chip_side[d], hf], near.at[n, d, hf], near_send.at[n, d, hf], near_recv.at[n, d, hf], sides[d]
        )

    def own_rows(m, n):
        return pltpu.make_async_copy(
            land.at[m, me, :, sl(n * cols, cols)], own_stage.at[n], own_sem.at[n]
        )

    def out_copy(m, n):
        return pltpu.make_async_copy(
            out_stage.at[n], (out_a, out_b)[m].at[:, sl(n * cols, cols)], stage_sem.at[n]
        )

    def back_pair(n):
        r_pair(n).start()

    def back_far(n):
        r_pair(n).wait()

        def body(k, carry):
            for hf in range(2):
                pair[n, k, hf] += partial[core, k, hf]
            return carry

        lax.fori_loop(jnp.int32(0), jnp.int32(n_chips), body, 0)
        for d in range(2):
            r_far(n, d).start()
        for d in range(2):
            r_near(n, d, 1 - d).start()

    def back_near(m, n):
        for d in range(2):
            r_far(n, d).wait_recv()
            pair[n, chip_side[d], d] += transit[n, d]
            r_near(n, d, d).start()
        own_rows(m, n).start()

    def back_out(m, n):
        for d in range(2):
            r_far(n, d).wait_send()
            for hf in range(2):
                r_near(n, d, hf).wait()
        own_rows(m, n).wait()
        if m == 1:
            out_copy(0, n).wait()
        for hf in range(2):
            part = slice(hf * half, (hf + 1) * half)
            total = pair[n, chip, hf] + near[n, 0, hf] + near[n, 1, hf]
            out_stage[n, :, part] = (own_stage[n, :, part].astype(F32) + total).astype(BF16)
        out_copy(m, n).start()

    for k in range(3):
        fetch('proj', jnp.int32(k))
    barrier = pltpu.get_barrier_semaphore()
    for k in range(1, n_devs):
        pl.semaphore_signal(
            barrier, inc=1, device_id={'ep': rem(me + k, n_devs)}, device_id_type=pl.DeviceIdType.MESH
        )
    attn_in = pltpu.make_async_copy(attn_b, rows.at[0, 0:tok_n], load_sem.at[0])
    h_in = pltpu.make_async_copy(h_b, rows.at[1, 0:tok_n], load_sem.at[1])
    x_in = pltpu.make_async_copy(x_a, rows.at[3, 0:tok_n], own_sem.at[0])
    attn_in.start()
    h_in.start()
    x_in.start()
    pl.semaphore_wait(barrier, n_devs - 1)

    def m_send(k):
        to = rem(me + k, n_devs)
        return remote(meta.at[to], table.at[me], meta_send.at[k], meta_recv.at[k], to)

    for k in range(1, n_devs):
        m_send(k).start()
    gather_start(0)
    table[me] = meta[me]
    x_in.wait()
    x_put = pltpu.make_async_copy(rows.at[3, 0:tok_n], land.at[0, me], own_sem.at[0])
    x_put.start()
    attn_in.wait()
    h_in.wait()

    def proj_tile(j, carry):
        arrive('proj', j)
        next_tile('proj', 'qkv', j)
        part = sl(j * cols, cols)
        got = jnp.dot(rows[0, 0:tok_n], wbuf[rem(j, SLOTS), :, 0:cols], preferred_element_type=F32).astype(BF16)
        rows[2, 0:tok_n, part] = (rows[1, 0:tok_n, part].astype(F32) + got.astype(F32)).astype(BF16)
        return carry

    lax.fori_loop(jnp.int32(0), jnp.int32(count['proj']), proj_tile, 0)
    mid_put = pltpu.make_async_copy(rows.at[2, 0:tok_n], land.at[1, me], own_sem.at[1])
    mid_put.start()

    def qkv_copy(j):
        return pltpu.make_async_copy(
            out_stage.at[rem(j, CHUNKS)], qkv.at[:, sl(j * cols, cols)], stage_sem.at[rem(j, CHUNKS)]
        )

    def qkv_tile(j, carry):
        arrive('qkv', j)
        next_tile('qkv', 'gate_up', j)

        @pl.when(j >= CHUNKS)
        def _():
            qkv_copy(j - CHUNKS).wait()

        got = jnp.dot(rows[1, 0:tok_n], wbuf[rem(j, SLOTS), :, 0:cols], preferred_element_type=F32)
        out_stage[rem(j, CHUNKS)] = got.astype(BF16)
        qkv_copy(j).start()

        @pl.when(j == count['qkv'] // 2)
        def _():
            gather_forward(0)

        return carry

    lax.fori_loop(jnp.int32(0), jnp.int32(count['qkv']), qkv_tile, 0)
    x_put.wait()
    mid_put.wait()
    for j in range(count['qkv'] - CHUNKS, count['qkv']):
        qkv_copy(jnp.int32(j)).wait()
    for k in range(1, n_devs):
        m_send(k).wait()
    make_mixer(0)
    gather_pass(0)
    gather_start(1)
    gather_near_done(0)

    for m in range(2):
        dispatch(m, 0, n_devs - 2)
        if m == 0:
            gather_pass_far(0)
            gather_done(0)
        dispatch(m, n_devs - 2, n_devs)
        if m == 1:
            make_mixer(1)
            back_far(jnp.int32(CHUNKS - 1))
            back_near(0, jnp.int32(1))

        def gu_expert(e, carry, m=m):
            def full_tile(t, carry):
                i = e * gu_tiles + t
                arrive('gate_up', i, 0)
                next_tile('gate_up', 'down', i)
                slot = rem(i, SLOTS)
                g = jnp.dot(rows[e], wbuf[slot, :, 0:WIDE], preferred_element_type=F32)
                u = jnp.dot(rows[e], wbuf[slot, :, WIDE : 2 * WIDE], preferred_element_type=F32)
                hidden[e, :, sl(t * WIDE, WIDE)] = (jax.nn.silu(g) * u).astype(BF16)
                return carry

            lax.fori_loop(jnp.int32(0), jnp.int32(n_full), full_tile, 0)
            i = e * gu_tiles + n_full
            arrive('gate_up', i, 1)
            next_tile('gate_up', 'down', i)
            gu = jnp.dot(rows[e], wbuf[rem(i, SLOTS), :, 0 : 2 * tail], preferred_element_type=F32)
            hidden[e, :, n_full * WIDE : ff] = (jax.nn.silu(gu[:, 0:tail]) * gu[:, tail : 2 * tail]).astype(BF16)

            if m == 0:
                events = {2: [lambda: gather_forward(1)], 4: [lambda: gather_pass(1)]}
            else:
                events = {
                    1: [lambda: back_near(0, jnp.int32(2))],
                    3: [lambda: back_out(0, jnp.int32(0))],
                    4: [lambda: back_near(0, jnp.int32(3))],
                    5: [lambda: back_out(0, jnp.int32(1))],
                    6: [lambda: back_out(0, jnp.int32(2))],
                    7: [lambda: back_out(0, jnp.int32(3))],
                }
            for at, steps in events.items():
                def run(steps=steps):
                    for step in steps:
                        step()
                pl.when(e == at)(run)
            return carry

        lax.fori_loop(jnp.int32(0), jnp.int32(local_n), gu_expert, 0)
        if m == 0:
            gather_pass_far(1)
        else:
            for dev in (partner, right, left):
                pl.semaphore_signal(credit, inc=1, device_id={'ep': dev}, device_id_type=pl.DeviceIdType.MESH)

        def down_chunk(n, carry, m=m):
            def tile(e, carry):
                i = n * local_n + e
                arrive('down', i)
                next_tile('down', 'gate_up' if m == 0 else None, i)
                y = jnp.dot(hidden[e], wbuf[rem(i, SLOTS), 0:ff, 0:cols], preferred_element_type=F32).astype(BF16)
                expert_out[:, pl.ds(pl.multiple_of(e * capacity, capacity), capacity), :] = y.reshape(
                    n_devs, capacity, cols
                )

                @pl.when((e == 2) & (n == 2))
                def _():
                    back_near(m, jnp.int32(0))

                @pl.when((e == 5) & (n >= 1))
                def _():
                    back_far(n - 1)

                return carry

            lax.fori_loop(jnp.int32(0), jnp.int32(local_n), tile, 0)

            def mix(s, carry):
                for hf in range(2):
                    ys = expert_out[s, :, hf * half : (hf + 1) * half]
                    got = jnp.dot(mixer[s], ys, preferred_element_type=F32)
                    partial[rem(s, 2), div(s, 2), hf] = (
                        got[0:tok_n] + got[tok_n : 2 * tok_n] + got[2 * tok_n : 3 * tok_n]
                    )
                return carry

            lax.fori_loop(jnp.int32(0), jnp.int32(n_devs), mix, 0)
            if m == 1:
                @pl.when(n == 0)
                def _():
                    pl.semaphore_wait(credit, 3)

            back_pair(n)
            return carry

        lax.fori_loop(jnp.int32(0), jnp.int32(CHUNKS), down_chunk, 0)
        if m == 0:
            gather_near_done(1)
            gather_done(1)

    back_near(1, jnp.int32(1))
    back_far(jnp.int32(CHUNKS - 1))
    back_near(1, jnp.int32(2))
    back_out(1, jnp.int32(0))
    back_near(1, jnp.int32(3))
    for n in range(1, CHUNKS):
        back_out(1, jnp.int32(n))
    for n in range(CHUNKS):
        out_copy(1, jnp.int32(n)).wait()


def own_table(route, gate, n_experts):
    tok_n = route.shape[0]
    hits = route.T[:, None, :] == jnp.arange(n_experts)[None, :, None]
    chosen = jnp.any(hits, axis=0)
    gates = jnp.sum(jnp.where(hits, gate.T[:, None, :], 0.0), axis=0)
    before = (jnp.arange(tok_n)[:, None] < jnp.arange(tok_n)[None, :]).astype(BF16)
    rank = jnp.dot(chosen.astype(BF16), before, preferred_element_type=F32)
    return jnp.where(chosen, rank, -1.0), gates


def solution(mesh):
    n_devs = mesh.shape['ep']

    def local_step(x_a, route_a, gate_a, h_b, attn_b, route_b, gate_b, w_qkv, w_o, w_gate, w_up, w_down):
        tok_n, dim = x_a.shape
        top_k = route_a.shape[1]
        local_n, _, ff = w_gate.shape
        n_experts = local_n * n_devs
        capacity = min(tok_n, 2 * ((tok_n * top_k + n_experts - 1) // n_experts))
        row_n, n_slots, cols = n_devs * capacity, local_n * capacity, dim // CHUNKS
        half, n_chips = cols // 2, n_devs // 2

        halves = []
        for route, gate in ((route_a, gate_a), (route_b, gate_b)):
            rank, gates = own_table(route, gate, n_experts)
            halves.append(
                jnp.concatenate(
                    [rank.reshape(n_devs, local_n, tok_n), gates.reshape(n_devs, local_n, tok_n)], axis=1
                )
            )
        meta = jnp.stack(halves, axis=1)

        any_spec = pl.BlockSpec(memory_space=pl.ANY)
        dma = pltpu.SemaphoreType.DMA

        def body(*refs):
            moe_kernel(capacity, *refs)

        flops = 2 * (6 * local_n * row_n * dim * ff + 8 * n_devs * n_slots * tok_n * dim) + 2 * tok_n * dim * 4 * dim
        out_a, out_b, qkv_b, _ = pl.pallas_call(
            body,
            in_specs=[any_spec, any_spec, any_spec, pl.BlockSpec(memory_space=pltpu.VMEM)] + [any_spec] * 5,
            out_specs=[any_spec] * 4,
            out_shape=[
                jax.ShapeDtypeStruct((tok_n, dim), BF16),
                jax.ShapeDtypeStruct((tok_n, dim), BF16),
                jax.ShapeDtypeStruct((tok_n, w_qkv.shape[1]), BF16),
                jax.ShapeDtypeStruct((2, n_devs, tok_n, dim), BF16),
            ],
            scratch_shapes=[
                pltpu.VMEM((SLOTS, dim, max(cols, 2 * WIDE)), BF16),
                pltpu.VMEM((local_n, row_n, dim), BF16),
                pltpu.VMEM((local_n, row_n, ff), BF16),
                pltpu.VMEM((2, tok_n, dim), BF16),
                pltpu.VMEM((n_devs, n_slots, cols), BF16),
                pltpu.VMEM((n_devs, 3 * tok_n, n_slots), BF16),
                pltpu.VMEM((2, n_chips, 2, tok_n, half), F32),
                pltpu.VMEM((CHUNKS, n_chips, 2, tok_n, half), F32),
                pltpu.VMEM((CHUNKS, 2, tok_n, half), F32),
                pltpu.VMEM((CHUNKS, 2, 2, tok_n, half), F32),
                pltpu.VMEM((CHUNKS, tok_n, cols), BF16),
                pltpu.VMEM((CHUNKS, tok_n, cols), BF16),
                pltpu.VMEM((n_devs, 2, 2 * local_n, tok_n), F32),
                dma((SLOTS, 2)),
                dma((2, 11)),
                dma((2, 11)),
                dma((n_devs,)),
                dma((n_devs,)),
                dma((2,)),
                dma((CHUNKS,)),
                dma((CHUNKS,)),
                dma((CHUNKS,)),
                dma((CHUNKS,)),
                dma((CHUNKS, 2)),
                dma((CHUNKS, 2)),
                dma((CHUNKS, 2, 2)),
                dma((CHUNKS, 2, 2)),
                pltpu.SemaphoreType.REGULAR,
            ],
            compiler_params=pltpu.CompilerParams(
                collective_id=0, has_side_effects=True, vmem_limit_bytes=VMEM_LIMIT
            ),
            cost_estimate=pl.CostEstimate(flops=flops, bytes_accessed=400_000_000, transcendentals=0),
            name="moe_step",
        )(x_a, h_b, attn_b, meta, w_qkv, w_o, w_gate, w_up, w_down)
        return out_a, out_b, qkv_b

    row_spec = P(('dp', 'ep'), None)
    full_spec = P(None, None)
    expert_spec = P('ep', None, None)
    return jax.shard_map(
        local_step,
        mesh=mesh,
        in_specs=(row_spec, row_spec, row_spec, row_spec, row_spec, row_spec, row_spec, full_spec, full_spec, expert_spec, expert_spec, expert_spec),
        out_specs=(row_spec, row_spec, row_spec),
        check_vma=False,
    )
```

time: 672 us -> 299 us (0.44)
  Pallas kernels: 0 us -> 285 us
  waiting for transfers between devices: 271 us -> 0 us
  matrix products: 240 us -> 0.31 us
  local copies, waits for them, and re-layouts: 72.6 us -> 8.49 us
  other arithmetic: 52.1 us -> 3.79 us
  starting transfers between devices: 28.2 us -> 0 us
    pallas_call x0 -> x1, Pallas kernels: none -> 285 us  [local_step(): pl.pallas_call(body, in_specs=[any_spec, any_spec, any_spec, pl.BlockSpec...]
    all_to_all x4 -> x0, waiting for transfers between devices: 271 us -> none  [the longest x2 140 us: moe_local(): recv_buf = lax.all_to_all(send_buf, 'ep', 1, 1, tiled=True)]
    dot_general x10 -> x2, matrix products: 240 us -> 0.31 us  [own_table(): rank = jnp.dot(chosen.astype(BF16), before, preferred_element_type=F32)]
    another operation x4 -> x2, other arithmetic: 36.3 us -> 0.74 us  [local_step(): meta = jnp.stack(halves, axis=1)]
    all_to_all x4 -> x0, local copies, waits for them, and re-layouts: 34.4 us -> none  [the longest x2 21.4 us: moe_local(): recv_buf = lax.all_to_all(send_buf, 'ep', 1, 1, tiled=True)]
    reshape x4 -> x0, local copies, waits for them, and re-layouts: 32.5 us -> none  [the longest x2 21.4 us: moe_local(): expert_out.reshape(local_n, n_devs, capacity, model_dim)]
    all_to_all x4 -> x0, starting transfers between devices: 28.2 us -> none  [the longest x2 14.7 us: moe_local(): recv_buf = lax.all_to_all(send_buf, 'ep', 1, 1, tiled=True)]
    convert_element_type x4 -> x0, other arithmetic: 8.42 us -> none  [the longest x2 8.35 us: moe_local(): return (tokens.astype(jnp.float32) + mixture).astype(jnp.bfloat16)]
  transfers between devices with their start and end apart: 4 -> 0, of which waited for: 4 -> 0; matrix products, arithmetic and copies ran while one was open for 43% -> 0% of each run, Pallas kernels for 0% -> 0%
where the time goes in v2:
time: 299 us; the launch traced here: 298 us
  Pallas kernels  285 us (95%)
  local copies, waits for them, and re-layouts  8.49 us (3%)
  other arithmetic  3.79 us (1%)
    pallas_call x1, Pallas kernels, local_step(): pl.pallas_call(body, in_specs=[any_spec, any_spec, any_spec, pl.BlockSpec...  285 us
    unnamed x3, local copies, waits for them, and re-layouts  8.49 us

profile of v2, /device:TPU:81, one launch (start us, length us, event | category | flops | bytes accessed | tf_op | source)
XLA Modules:
  0.0 298.3 jit_solution(15027463980975813714)
XLA Ops:
  0.6 0.8 fusion.3
  1.4 0.8 fusion.2
  2.1 0.2 fusion.1
  2.3 0.2 fusion
  2.5 0.8 select_reduce_fusion.1
  3.2 0.8 select_reduce_fusion
  4.0 0.7 pad_maximum_fusion.refs_3_
  4.7 285.0 %moe_step.1 = (bf16[256,2048]{1,0:T(8,128)(2,1)}, bf16[256,2048]{1,0:T(8,128)(2,1)}, bf16[256,6144]{1,0:T(8,128)(2,1)}, bf16[2,8,256,2048]{3,2,1,0:T(8,128)(2,1)}) custom-call(bf16[256,2048]{1,0:T(8,128)(2,1)} %refs_0_.1, bf16[256,2048]{1,0:T(8,128)(2,1)} %refs_1_.1, bf16[256,2048]{1,0:T(8,128)(2,1)} %refs_2_.1, f32[8,2,16,256]{3,2,1,0:T(8,128)} %pad_maximum_fusion.refs_3_, ...), custom_call_target="tpu_custom_call" | custom-call | flops 140660178944 | bytes 400000000 | tf_op jit(solution)/shard_map/moe_step/pallas_call | solution.py:522
  289.8 2.3 copy.18
  292.1 2.3 copy.19
  294.4 3.9 %copy.20 = bf16[256,6144]{1,0:T(8,128)(2,1)} copy(bf16[256,6144]{1,0:T(8,128)(2,1)} %get-tuple-element.16) | data formatting | bytes 6291456
  (1 shorter events, 0.0 us)

commit v3 on v2

--- a/solution.py
+++ b/solution.py
@@ -9,7 +9,7 @@
 BF16 = jnp.bfloat16
 VMEM_LIMIT = 67_000_000
 WIDE = 256
-SLOTS = 4
+SLOTS = 3
 CHUNKS = 4
 
 
@@ -23,9 +23,9 @@
 
 def moe_kernel(
     capacity,
-    x_a, h_b, attn_b, meta, w_qkv, w_o, w_gate, w_up, w_down,
+    x_a, h_b, attn_b, route_a, gate_a, route_b, gate_b, w_qkv, w_o, w_gate, w_up, w_down,
     out_a, out_b, qkv, land,
-    wbuf, rows, hidden, src_rows, expert_out, mixer, partial, pair, transit, near, out_stage, own_stage, table,
+    wbuf, rows, hidden, meta, expert_out, mixer, partial, pair, transit, near, out_stage, own_stage, table,
     w_sem, gather_send, gather_recv, meta_send, meta_recv, load_sem, stage_sem, own_sem,
     pair_send, pair_recv, far_send, far_recv, near_send, near_recv, credit,
 ):
@@ -58,51 +58,81 @@
     def sl(start, size):
         return pl.ds(pl.multiple_of(start, size), size)
 
-    def tile_copies(phase, i):
-        slot = rem(i, SLOTS)
-        if phase in ('proj', 'qkv'):
-            w = w_o if phase == 'proj' else w_qkv
-            return ((None, [(w.at[:, sl(i * cols, cols)], wbuf.at[slot, :, 0:cols], w_sem.at[slot, 0])]),)
-        if phase == 'down':
-            n, e = div(i, local_n), rem(i, local_n)
-            return ((None, [(w_down.at[e, :, sl(n * cols, cols)], wbuf.at[slot, 0:ff, 0:cols], w_sem.at[slot, 0])]),)
-        e, t = div(i, gu_tiles), rem(i, gu_tiles)
-        full = [
-            (w_gate.at[e, :, sl(t * WIDE, WIDE)], wbuf.at[slot, :, 0:WIDE], w_sem.at[slot, 0]),
-            (w_up.at[e, :, sl(t * WIDE, WIDE)], wbuf.at[slot, :, WIDE : 2 * WIDE], w_sem.at[slot, 1]),
-        ]
-        part = [
-            (w_gate.at[e, :, n_full * WIDE : ff], wbuf.at[slot, :, 0:tail], w_sem.at[slot, 0]),
-            (w_up.at[e, :, n_full * WIDE : ff], wbuf.at[slot, :, tail : 2 * tail], w_sem.at[slot, 1]),
-        ]
-        return ((t < n_full, full), (t == n_full, part))
-
-    def fetch(phase, i):
-        for cond, copies in tile_copies(phase, i):
-            def go(copies=copies):
-                for c in copies:
-                    pltpu.make_async_copy(*c).start()
-            if cond is None:
-                go()
+    pairs_of = {'proj': CHUNKS // 2, 'qkv': qkv.shape[1] // cols // 2, 'down': CHUNKS * local_n // 2}
+    gu_pairs = gu_tiles // 2
+    pairs_of['gate_up'] = local_n * gu_pairs
+    stream, total = [], 0
+    for kind in ('proj', 'qkv', 'gate_up', 'down', 'gate_up', 'down'):
+        stream.append((kind, total, pairs_of[kind]))
+        total += pairs_of[kind]
+
+    def slot_of(ph, q):
+        return rem(q + stream[ph][1], SLOTS)
+
+    def tile_copies(ph, q, r=0):
+        kind = stream[ph][0]
+        slot = slot_of(ph, q * gu_pairs + r if kind == 'gate_up' else q)
+        out = []
+        for k in range(2):
+            buf, sem = wbuf.at[slot, k], w_sem.at[slot, k]
+            if kind in ('proj', 'qkv'):
+                w = w_o if kind == 'proj' else w_qkv
+                out.append((w.at[:, sl((2 * q + k) * cols, cols)], buf.at[:, 0:cols], sem.at[0]))
+            elif kind == 'down':
+                n, e = div(q, local_n // 2), rem(q, local_n // 2) * 2 + k
+                out.append((w_down.at[e, :, sl(n * cols, cols)], buf.at[0:ff, 0:cols], sem.at[0]))
             else:
-                pl.when(cond)(go)
-
-    def arrive(phase, i, which=0):
-        for c in tile_copies(phase, i)[which][1]:
+                t = 2 * r + k
+                lo, size = t * WIDE, WIDE if t < n_full else tail
+                out.append((w_gate.at[q, :, lo : lo + size], buf.at[:, 0:size], sem.at[0]))
+                out.append((w_up.at[q, :, lo : lo + size], buf.at[:, size : 2 * size], sem.at[1]))
+        return out
+
+    def fetch(ph, q, r=0):
+        for c in tile_copies(ph, q, r):
+            pltpu.make_async_copy(*c).start()
+
+    def fetch_pair(ph, i):
+        kind = stream[ph][0]
+        if kind == 'gate_up':
+            fetch(ph, jnp.int32(i // gu_pairs), i % gu_pairs)
+        else:
+            fetch(ph, jnp.int32(i))
+
+    def arrive(ph, q, r=0):
+        for c in tile_copies(ph, q, r):
             pltpu.make_async_copy(*c).wait()
 
-    count = {'proj': CHUNKS, 'qkv': qkv.shape[1] // cols, 'gate_up': local_n * gu_tiles, 'down': CHUNKS * local_n}
     ahead = SLOTS - 1
 
-    def next_tile(phase, following, i):
-        @pl.when(i + ahead < count[phase])
+    def next_pair(ph, q):
+        n = stream[ph][2]
+
+        @pl.when(q + ahead < n)
         def _():
-            fetch(phase, i + ahead)
-
-        if following is not None:
-            @pl.when(i + ahead >= count[phase])
-            def _():
-                fetch(following, i + ahead - count[phase])
+            fetch(ph, q + ahead)
+
+        if ph + 1 < len(stream):
+            for k in range(ahead):
+                @pl.when(q == n - ahead + k)
+                def _(k=k):
+                    fetch_pair(ph + 1, k)
+
+    def next_pair_gu(ph, e, r):
+        if r + ahead < gu_pairs:
+            fetch(ph, e, r + ahead)
+            return
+        over = r + ahead - gu_pairs
+        step, pos = 1 + over // gu_pairs, over % gu_pairs
+
+        @pl.when(e + step < local_n)
+        def _():
+            fetch(ph, e + step, pos)
+
+        for k in range(ahead):
+            @pl.when(e * gu_pairs + r + ahead == stream[ph][2] + k)
+            def _(k=k):
+                fetch_pair(ph + 1, k)
 
     def own(m):
         return x_a if m == 0 else land.at[m, me]
@@ -173,8 +203,24 @@
         off = kk + div(kk, 2) - 2 * div(kk, 3)
         return 2 * rem(chip + off, n_chips) + rem(k, 2)
 
-    def load(m, k):
-        return pltpu.make_async_copy(land.at[m, source_at(k)], src_rows.at[rem(k, 2)], load_sem.at[rem(k, 2)])
+    class load:
+        def __init__(self, m, k):
+            self.copies = [
+                pltpu.make_async_copy(
+                    land.at[m, source_at(k), :, j * cols : (j + 1) * cols],
+                    expert_out.at[CHUNKS * rem(k, 2) + j, 0:tok_n],
+                    load_sem.at[rem(k, 2), j],
+                )
+                for j in range(CHUNKS)
+            ]
+
+        def start(self):
+            for c in self.copies:
+                c.start()
+
+        def wait(self):
+            for c in self.copies:
+                c.wait()
 
     def dispatch(m, lo, hi):
         load(m, jnp.int32(lo)).start()
@@ -193,7 +239,7 @@
             )
             for j in range(CHUNKS):
                 part = slice(j * cols, (j + 1) * cols)
-                got = jnp.dot(pick, src_rows[slot, :, part], preferred_element_type=F32).astype(BF16)
+                got = jnp.dot(pick, expert_out[CHUNKS * slot + j, 0:tok_n], preferred_element_type=F32).astype(BF16)
                 for e in range(local_n):
                     rows[e, pl.ds(pl.multiple_of(s * capacity, capacity), capacity), part] = got[
                         e * capacity : (e + 1) * capacity
@@ -294,15 +340,15 @@
             out_stage[n, :, part] = (own_stage[n, :, part].astype(F32) + total).astype(BF16)
         out_copy(m, n).start()
 
-    for k in range(3):
-        fetch('proj', jnp.int32(k))
+    for k in range(ahead):
+        fetch_pair(0, k)
     barrier = pltpu.get_barrier_semaphore()
     for k in range(1, n_devs):
         pl.semaphore_signal(
             barrier, inc=1, device_id={'ep': rem(me + k, n_devs)}, device_id_type=pl.DeviceIdType.MESH
         )
-    attn_in = pltpu.make_async_copy(attn_b, rows.at[0, 0:tok_n], load_sem.at[0])
-    h_in = pltpu.make_async_copy(h_b, rows.at[1, 0:tok_n], load_sem.at[1])
+    attn_in = pltpu.make_async_copy(attn_b, rows.at[0, 0:tok_n], load_sem.at[0, 0])
+    h_in = pltpu.make_async_copy(h_b, rows.at[1, 0:tok_n], load_sem.at[1, 0])
     x_in = pltpu.make_async_copy(x_a, rows.at[3, 0:tok_n], own_sem.at[0])
     attn_in.start()
     h_in.start()
@@ -313,9 +359,26 @@
         to = rem(me + k, n_devs)
         return remote(meta.at[to], table.at[me], meta_send.at[k], meta_recv.at[k], to)
 
+    gather_start(0)
+    n_experts = n_devs * local_n
+    before = jnp.where(
+        lax.broadcasted_iota(jnp.int32, (tok_n, tok_n), 0) < lax.broadcasted_iota(jnp.int32, (tok_n, tok_n), 1), 1.0, 0.0
+    ).astype(BF16)
+    ids = lax.broadcasted_iota(jnp.int32, (n_experts, tok_n), 0)
+    for m, (route, gate) in enumerate(((route_a, gate_a), (route_b, gate_b))):
+        chosen = jnp.zeros((n_experts, tok_n), F32)
+        gates = jnp.zeros((n_experts, tok_n), F32)
+        for j in range(route.shape[0]):
+            hit = route[j : j + 1] == ids
+            chosen = jnp.where(hit, 1.0, chosen)
+            gates = jnp.where(hit, gate[j : j + 1], gates)
+        rank = jnp.dot(chosen.astype(BF16), before, preferred_element_type=F32)
+        rank = jnp.where(chosen > 0.5, rank, -1.0)
+        for d in range(n_devs):
+            meta[d, m, 0:local_n] = rank[d * local_n : (d + 1) * local_n]
+            meta[d, m, local_n : 2 * local_n] = gates[d * local_n : (d + 1) * local_n]
     for k in range(1, n_devs):
         m_send(k).start()
-    gather_start(0)
     table[me] = meta[me]
     x_in.wait()
     x_put = pltpu.make_async_copy(rows.at[3, 0:tok_n], land.at[0, me], own_sem.at[0])
@@ -323,15 +386,17 @@
     attn_in.wait()
     h_in.wait()
 
-    def proj_tile(j, carry):
-        arrive('proj', j)
-        next_tile('proj', 'qkv', j)
-        part = sl(j * cols, cols)
-        got = jnp.dot(rows[0, 0:tok_n], wbuf[rem(j, SLOTS), :, 0:cols], preferred_element_type=F32).astype(BF16)
-        rows[2, 0:tok_n, part] = (rows[1, 0:tok_n, part].astype(F32) + got.astype(F32)).astype(BF16)
+    def proj_pair(q, carry):
+        arrive(0, q)
+        next_pair(0, q)
+        slot = slot_of(0, q)
+        for k in range(2):
+            part = sl((2 * q + k) * cols, cols)
+            got = jnp.dot(rows[0, 0:tok_n], wbuf[slot, k, :, 0:cols], preferred_element_type=F32).astype(BF16)
+            rows[2, 0:tok_n, part] = (rows[1, 0:tok_n, part].astype(F32) + got.astype(F32)).astype(BF16)
         return carry
 
-    lax.fori_loop(jnp.int32(0), jnp.int32(count['proj']), proj_tile, 0)
+    lax.fori_loop(jnp.int32(0), jnp.int32(stream[0][2]), proj_pair, 0)
     mid_put = pltpu.make_async_copy(rows.at[2, 0:tok_n], land.at[1, me], own_sem.at[1])
     mid_put.start()
 
@@ -340,28 +405,34 @@
             out_stage.at[rem(j, CHUNKS)], qkv.at[:, sl(j * cols, cols)], stage_sem.at[rem(j, CHUNKS)]
         )
 
-    def qkv_tile(j, carry):
-        arrive('qkv', j)
-        next_tile('qkv', 'gate_up', j)
-
-        @pl.when(j >= CHUNKS)
-        def _():
-            qkv_copy(j - CHUNKS).wait()
-
-        got = jnp.dot(rows[1, 0:tok_n], wbuf[rem(j, SLOTS), :, 0:cols], preferred_element_type=F32)
-        out_stage[rem(j, CHUNKS)] = got.astype(BF16)
-        qkv_copy(j).start()
-
-        @pl.when(j == count['qkv'] // 2)
+    def qkv_pair(q, carry):
+        arrive(1, q)
+        next_pair(1, q)
+        slot = slot_of(1, q)
+        for k in range(2):
+            j = 2 * q + k
+
+            @pl.when(j >= CHUNKS)
+            def _(j=j):
+                qkv_copy(j - CHUNKS).wait()
+
+        for k in range(2):
+            j = 2 * q + k
+            got = jnp.dot(rows[1, 0:tok_n], wbuf[slot, k, :, 0:cols], preferred_element_type=F32)
+            out_stage[rem(j, CHUNKS)] = got.astype(BF16)
+        for k in range(2):
+            qkv_copy(2 * q + k).start()
+
+        @pl.when(q == stream[1][2] // 2)
         def _():
             gather_forward(0)
 
         return carry
 
-    lax.fori_loop(jnp.int32(0), jnp.int32(count['qkv']), qkv_tile, 0)
+    lax.fori_loop(jnp.int32(0), jnp.int32(stream[1][2]), qkv_pair, 0)
     x_put.wait()
     mid_put.wait()
-    for j in range(count['qkv'] - CHUNKS, count['qkv']):
+    for j in range(2 * stream[1][2] - CHUNKS, 2 * stream[1][2]):
         qkv_copy(jnp.int32(j)).wait()
     for k in range(1, n_devs):
         m_send(k).wait()
@@ -382,22 +453,22 @@
             back_near(0, jnp.int32(1))
 
         def gu_expert(e, carry, m=m):
-            def full_tile(t, carry):
-                i = e * gu_tiles + t
-                arrive('gate_up', i, 0)
-                next_tile('gate_up', 'down', i)
-                slot = rem(i, SLOTS)
-                g = jnp.dot(rows[e], wbuf[slot, :, 0:WIDE], preferred_element_type=F32)
-                u = jnp.dot(rows[e], wbuf[slot, :, WIDE : 2 * WIDE], preferred_element_type=F32)
-                hidden[e, :, sl(t * WIDE, WIDE)] = (jax.nn.silu(g) * u).astype(BF16)
-                return carry
-
-            lax.fori_loop(jnp.int32(0), jnp.int32(n_full), full_tile, 0)
-            i = e * gu_tiles + n_full
-            arrive('gate_up', i, 1)
-            next_tile('gate_up', 'down', i)
-            gu = jnp.dot(rows[e], wbuf[rem(i, SLOTS), :, 0 : 2 * tail], preferred_element_type=F32)
-            hidden[e, :, n_full * WIDE : ff] = (jax.nn.silu(gu[:, 0:tail]) * gu[:, tail : 2 * tail]).astype(BF16)
+            ph = 2 + 2 * m
+            for r in range(gu_pairs):
+                arrive(ph, e, r)
+                next_pair_gu(ph, e, r)
+                slot = slot_of(ph, e * gu_pairs + r)
+                for k in range(2):
+                    t = 2 * r + k
+                    if t < n_full:
+                        g = jnp.dot(rows[e], wbuf[slot, k, :, 0:WIDE], preferred_element_type=F32)
+                        u = jnp.dot(rows[e], wbuf[slot, k, :, WIDE : 2 * WIDE], preferred_element_type=F32)
+                        hidden[e, :, t * WIDE : (t + 1) * WIDE] = (jax.nn.silu(g) * u).astype(BF16)
+                    else:
+                        gu = jnp.dot(rows[e], wbuf[slot, k, :, 0 : 2 * tail], preferred_element_type=F32)
+                        hidden[e, :, n_full * WIDE : ff] = (
+                            jax.nn.silu(gu[:, 0:tail]) * gu[:, tail : 2 * tail]
+                        ).astype(BF16)
 
             if m == 0:
                 events = {2: [lambda: gather_forward(1)], 4: [lambda: gather_pass(1)]}
@@ -425,37 +496,41 @@
                 pl.semaphore_signal(credit, inc=1, device_id={'ep': dev}, device_id_type=pl.DeviceIdType.MESH)
 
         def down_chunk(n, carry, m=m):
-            def tile(e, carry):
-                i = n * local_n + e
-                arrive('down', i)
-                next_tile('down', 'gate_up' if m == 0 else None, i)
-                y = jnp.dot(hidden[e], wbuf[rem(i, SLOTS), 0:ff, 0:cols], preferred_element_type=F32).astype(BF16)
-                expert_out[:, pl.ds(pl.multiple_of(e * capacity, capacity), capacity), :] = y.reshape(
-                    n_devs, capacity, cols
-                )
-
-                @pl.when((e == 2) & (n == 2))
+            ph = 3 + 2 * m
+
+            def pair_of(r, carry):
+                q = n * (local_n // 2) + r
+                arrive(ph, q)
+                next_pair(ph, q)
+                slot = slot_of(ph, q)
+                for k in range(2):
+                    e = 2 * r + k
+                    y = jnp.dot(hidden[e], wbuf[slot, k, 0:ff, 0:cols], preferred_element_type=F32).astype(BF16)
+                    expert_out[:, pl.ds(pl.multiple_of(e * capacity, capacity), capacity), :] = y.reshape(
+                        n_devs, capacity, cols
+                    )
+
+                @pl.when((r == 1) & (n == 2))
                 def _():
                     back_near(m, jnp.int32(0))
 
-                @pl.when((e == 5) & (n >= 1))
+                @pl.when((r == 2) & (n >= 1))
                 def _():
                     back_far(n - 1)
 
                 return carry
 
-            lax.fori_loop(jnp.int32(0), jnp.int32(local_n), tile, 0)
-
-            def mix(s, carry):
-                for hf in range(2):
-                    ys = expert_out[s, :, hf * half : (hf + 1) * half]
-                    got = jnp.dot(mixer[s], ys, preferred_element_type=F32)
-                    partial[rem(s, 2), div(s, 2), hf] = (
-                        got[0:tok_n] + got[tok_n : 2 * tok_n] + got[2 * tok_n : 3 * tok_n]
-                    )
+            lax.fori_loop(jnp.int32(0), jnp.int32(local_n // 2), pair_of, 0)
+
+            def mix(r, carry):
+                for k in range(2):
+                    for hf in range(2):
+                        ys = expert_out[2 * r + k, :, hf * half : (hf + 1) * half]
+                        got = jnp.dot(mixer[2 * r + k], ys, preferred_element_type=F32)
+                        partial[k, r, hf] = got[0:tok_n] + got[tok_n : 2 * tok_n] + got[2 * tok_n : 3 * tok_n]
                 return carry
 
-            lax.fori_loop(jnp.int32(0), jnp.int32(n_devs), mix, 0)
+            lax.fori_loop(jnp.int32(0), jnp.int32(n_devs // 2), mix, 0)
             if m == 1:
                 @pl.when(n == 0)
                 def _():
@@ -480,14 +555,36 @@
         out_copy(1, jnp.int32(n)).wait()
 
 
-def own_table(route, gate, n_experts):
-    tok_n = route.shape[0]
-    hits = route.T[:, None, :] == jnp.arange(n_experts)[None, :, None]
-    chosen = jnp.any(hits, axis=0)
-    gates = jnp.sum(jnp.where(hits, gate.T[:, None, :], 0.0), axis=0)
-    before = (jnp.arange(tok_n)[:, None] < jnp.arange(tok_n)[None, :]).astype(BF16)
-    rank = jnp.dot(chosen.astype(BF16), before, preferred_element_type=F32)
-    return jnp.where(chosen, rank, -1.0), gates
+def hand_over_kernel(*refs):
+    ins, outs, bufs, sems = refs[0:3], refs[3:6], refs[6:9], refs[9]
+    pieces = sems.shape[2]
+    size = ins[0].shape[0] // pieces
+
+    def move(src, dst, i, p, way):
+        at = pl.ds(p * size, size)
+        return pltpu.make_async_copy(src.at[at], dst.at[at], sems.at[way, i, p])
+
+    todo = [(i, p) for i in range(3) for p in range(pieces)]
+    for i, p in todo:
+        move(ins[i], bufs[i], i, p, 0).start()
+    for i, p in todo:
+        move(ins[i], bufs[i], i, p, 0).wait()
+        move(bufs[i], outs[i], i, p, 1).start()
+    for i, p in todo:
+        move(bufs[i], outs[i], i, p, 1).wait()
+
+
+def hand_over(arrays):
+    any_spec = pl.BlockSpec(memory_space=pl.ANY)
+    return pl.pallas_call(
+        hand_over_kernel,
+        in_specs=[any_spec] * 3,
+        out_specs=[any_spec] * 3,
+        out_shape=[jax.ShapeDtypeStruct(a.shape, a.dtype) for a in arrays],
+        scratch_shapes=[pltpu.VMEM(a.shape, a.dtype) for a in arrays] + [pltpu.SemaphoreType.DMA((2, 3, 4))],
+        compiler_params=pltpu.CompilerParams(vmem_limit_bytes=VMEM_LIMIT),
+        name="hand_over",
+    )(*arrays)
 
 
 def solution(mesh):
@@ -502,16 +599,6 @@
         row_n, n_slots, cols = n_devs * capacity, local_n * capacity, dim // CHUNKS
         half, n_chips = cols // 2, n_devs // 2
 
-        halves = []
-        for route, gate in ((route_a, gate_a), (route_b, gate_b)):
-            rank, gates = own_table(route, gate, n_experts)
-            halves.append(
-                jnp.concatenate(
-                    [rank.reshape(n_devs, local_n, tok_n), gates.reshape(n_devs, local_n, tok_n)], axis=1
-                )
-            )
-        meta = jnp.stack(halves, axis=1)
-
         any_spec = pl.BlockSpec(memory_space=pl.ANY)
         dma = pltpu.SemaphoreType.DMA
 
@@ -521,7 +608,7 @@
         flops = 2 * (6 * local_n * row_n * dim * ff + 8 * n_devs * n_slots * tok_n * dim) + 2 * tok_n * dim * 4 * dim
         out_a, out_b, qkv_b, _ = pl.pallas_call(
             body,
-            in_specs=[any_spec, any_spec, any_spec, pl.BlockSpec(memory_space=pltpu.VMEM)] + [any_spec] * 5,
+            in_specs=[any_spec] * 3 + [pl.BlockSpec(memory_space=pltpu.VMEM)] * 4 + [any_spec] * 5,
             out_specs=[any_spec] * 4,
             out_shape=[
                 jax.ShapeDtypeStruct((tok_n, dim), BF16),
@@ -530,10 +617,10 @@
                 jax.ShapeDtypeStruct((2, n_devs, tok_n, dim), BF16),
             ],
             scratch_shapes=[
-                pltpu.VMEM((SLOTS, dim, max(cols, 2 * WIDE)), BF16),
+                pltpu.VMEM((SLOTS, 2, dim, max(cols, 2 * WIDE)), BF16),
                 pltpu.VMEM((local_n, row_n, dim), BF16),
                 pltpu.VMEM((local_n, row_n, ff), BF16),
-                pltpu.VMEM((2, tok_n, dim), BF16),
+                pltpu.VMEM((n_devs, 2, 2 * local_n, tok_n), F32),
                 pltpu.VMEM((n_devs, n_slots, cols), BF16),
                 pltpu.VMEM((n_devs, 3 * tok_n, n_slots), BF16),
                 pltpu.VMEM((2, n_chips, 2, tok_n, half), F32),
@@ -543,12 +630,12 @@
                 pltpu.VMEM((CHUNKS, tok_n, cols), BF16),
                 pltpu.VMEM((CHUNKS, tok_n, cols), BF16),
                 pltpu.VMEM((n_devs, 2, 2 * local_n, tok_n), F32),
-                dma((SLOTS, 2)),
+                dma((SLOTS, 2, 2)),
                 dma((2, 11)),
                 dma((2, 11)),
                 dma((n_devs,)),
                 dma((n_devs,)),
-                dma((2,)),
+                dma((2, CHUNKS)),
                 dma((CHUNKS,)),
                 dma((CHUNKS,)),
                 dma((CHUNKS,)),
@@ -564,8 +651,8 @@
             ),
             cost_estimate=pl.CostEstimate(flops=flops, bytes_accessed=400_000_000, transcendentals=0),
             name="moe_step",
-        )(x_a, h_b, attn_b, meta, w_qkv, w_o, w_gate, w_up, w_down)
-        return out_a, out_b, qkv_b
+        )(x_a, h_b, attn_b, route_a.T, gate_a.T, route_b.T, gate_b.T, w_qkv, w_o, w_gate, w_up, w_down)
+        return tuple(hand_over((out_a, out_b, qkv_b)))
 
     row_spec = P(('dp', 'ep'), None)
     full_spec = P(None, None)

time: 299 us -> 289 us (0.967)
  local copies, waits for them, and re-layouts: 8.49 us -> 0 us
  other arithmetic: 3.79 us -> 0 us
  Pallas kernels: 285 us -> 288 us
    unnamed x3 -> x0, local copies, waits for them, and re-layouts: 8.49 us -> none
    pallas_call x1 -> x2, Pallas kernels: 285 us -> 288 us  [the longest x1 283 us: local_step(): pl.pallas_call(body, in_specs=[any_spec] * 3 + [pl.BlockSpec(memory_space...]
where the time goes in v3:
time: 289 us; the launch traced here: 288 us
  Pallas kernels  288 us (100%)
    pallas_call x1, Pallas kernels, local_step(): pl.pallas_call(body, in_specs=[any_spec] * 3 + [pl.BlockSpec(memory_space...  283 us

profile of v3, /device:TPU:81, one launch (start us, length us, event | category | flops | bytes accessed | tf_op | source)
XLA Modules:
  0.0 288.4 jit_solution(14835355976919881204)
XLA Ops:
  0.6 282.7 %moe_step.1 = (bf16[256,2048]{1,0:T(8,128)(2,1)}, bf16[256,2048]{1,0:T(8,128)(2,1)}, bf16[256,6144]{1,0:T(8,128)(2,1)}, bf16[2,8,256,2048]{3,2,1,0:T(8,128)(2,1)}) custom-call(bf16[256,2048]{1,0:T(8,128)(2,1)} %refs_0_.1, bf16[256,2048]{1,0:T(8,128)(2,1)} %refs_1_.1, bf16[256,2048]{1,0:T(8,128)(2,1)} %refs_2_.1, s32[6,256]{1,0:T(8,128)} %bitcast.4, ...), custom_call_target="tpu_custom_call" | custom-call | flops 140660178944 | bytes 400000000 | tf_op jit(solution)/shard_map/moe_step/pallas_call | solution.py:609
  283.4 4.9 %hand_over.1 = (bf16[256,2048]{1,0:T(8,128)(2,1)}, bf16[256,2048]{1,0:T(8,128)(2,1)}, bf16[256,6144]{1,0:T(8,128)(2,1)}) custom-call(bf16[256,2048]{1,0:T(8,128)(2,1)} %get-tuple-element.6.refs_0_, bf16[256,2048]{1,0:T(8,128)(2,1)} %get-tuple-element.7.refs_1_, bf16[256,6144]{1,0:T(8,128)(2,1)} %get-tuple-element.8.refs_2_), custom_call_target="tpu_custom_call" | custom-call | tf_op jit(solution)/shard_map/hand_over/pallas_call | solution.py:579

commit v4 on v3

--- a/solution.py
+++ b/solution.py
@@ -24,10 +24,10 @@
 def moe_kernel(
     capacity,
     x_a, h_b, attn_b, route_a, gate_a, route_b, gate_b, w_qkv, w_o, w_gate, w_up, w_down,
-    out_a, out_b, qkv, land,
+    out, qkv, land,
     wbuf, rows, hidden, meta, expert_out, mixer, partial, pair, transit, near, out_stage, own_stage, table,
     w_sem, gather_send, gather_recv, meta_send, meta_recv, load_sem, stage_sem, own_sem,
-    pair_send, pair_recv, far_send, far_recv, near_send, near_recv, credit,
+    pair_send, pair_recv, far_send, far_recv, near_send, near_recv, ring_credit, pair_credit,
 ):
     n_devs = land.shape[1]
     n_chips = n_devs // 2
@@ -62,7 +62,7 @@
     gu_pairs = gu_tiles // 2
     pairs_of['gate_up'] = local_n * gu_pairs
     stream, total = [], 0
-    for kind in ('proj', 'qkv', 'gate_up', 'down', 'gate_up', 'down'):
+    for kind in ('proj', 'qkv') + ('gate_up', 'down') * 3:
         stream.append((kind, total, pairs_of[kind]))
         total += pairs_of[kind]
 
@@ -177,19 +177,18 @@
             g_near(m, d, 1 - d).wait_recv()
             g_pass(m, d).start()
 
-    def gather_near_done(m):
-        g_partner(m).wait_recv()
-        for d in range(2):
-            g_pass(m, d).wait_recv()
-
     def gather_pass_far(m):
         for d in range(2):
             g_forward(m, d).wait_recv()
             g_pass_far(m, d).start()
 
-    def gather_done(m):
+    def gather_from_partner(m):
+        g_partner(m).wait_recv()
         for d in range(2):
+            g_pass(m, d).wait_recv()
             g_pass_far(m, d).wait_recv()
+
+    def gather_sent(m):
         g_partner(m).wait_send()
         for d in range(2):
             g_near(m, d, 0).wait_send()
@@ -198,16 +197,33 @@
             g_pass(m, d).wait_send()
             g_pass_far(m, d).wait_send()
 
-    def source_at(k):
-        kk = div(k, 2)
-        off = kk + div(kk, 2) - 2 * div(kk, 3)
-        return 2 * rem(chip + off, n_chips) + rem(k, 2)
+    def on_core(c, *steps):
+        @pl.when(core == c)
+        def _():
+            for step in steps:
+                step()
+
+    n_pass = 3
+    sources = [n_chips, 2 * n_chips, n_chips]
+    members = [(0,), (0, 1), (1,)]
+
+    def batch_at(ps, t):
+        return div(t, n_chips) if ps == 1 else jnp.int32(ps // 2)
+
+    def core_at(ps, t):
+        return 1 - div(t, n_chips) if ps == 1 else jnp.int32(ps // 2)
+
+    def source_at(ps, t):
+        return 2 * rem(t, n_chips) + core_at(ps, t)
+
+    def my_batch(ps):
+        return 1 - core if ps == 1 else jnp.int32(ps // 2)
 
     class load:
-        def __init__(self, m, k):
+        def __init__(self, ps, k):
             self.copies = [
                 pltpu.make_async_copy(
-                    land.at[m, source_at(k), :, j * cols : (j + 1) * cols],
+                    land.at[batch_at(ps, k), source_at(ps, k), :, j * cols : (j + 1) * cols],
                     expert_out.at[CHUNKS * rem(k, 2) + j, 0:tok_n],
                     load_sem.at[rem(k, 2), j],
                 )
@@ -222,17 +238,18 @@
             for c in self.copies:
                 c.wait()
 
-    def dispatch(m, lo, hi):
-        load(m, jnp.int32(lo)).start()
+    def dispatch(ps):
+        hi = sources[ps]
+        load(ps, jnp.int32(0)).start()
 
         def body(k, carry):
             @pl.when(k + 1 < hi)
             def _():
-                load(m, k + 1).start()
-
-            s, slot = source_at(k), rem(k, 2)
-            load(m, k).wait()
-            rank = table[s, m, 0:local_n]
+                load(ps, k + 1).start()
+
+            slot = rem(k, 2)
+            load(ps, k).wait()
+            rank = table[source_at(ps, k), batch_at(ps, k), 0:local_n]
             slots = lax.broadcasted_iota(jnp.int32, (capacity, tok_n), 0).astype(F32)
             pick = jnp.concatenate(
                 [jnp.where(rank[e : e + 1] == slots, 1.0, 0.0).astype(BF16) for e in range(local_n)], axis=0
@@ -241,14 +258,14 @@
                 part = slice(j * cols, (j + 1) * cols)
                 got = jnp.dot(pick, expert_out[CHUNKS * slot + j, 0:tok_n], preferred_element_type=F32).astype(BF16)
                 for e in range(local_n):
-                    rows[e, pl.ds(pl.multiple_of(s * capacity, capacity), capacity), part] = got[
+                    rows[e, pl.ds(pl.multiple_of(k * capacity, capacity), capacity), part] = got[
                         e * capacity : (e + 1) * capacity
                     ]
             return carry
 
-        lax.fori_loop(jnp.int32(lo), jnp.int32(hi), body, 0)
-
-    def make_mixer(m):
+        lax.fori_loop(jnp.int32(0), jnp.int32(hi), body, 0)
+
+    def make_mixer(ps):
         lane = lax.broadcasted_iota(jnp.int32, (2 * local_n, n_slots), 1)
         line = lax.broadcasted_iota(jnp.int32, (2 * local_n, n_slots), 0)
 
@@ -265,7 +282,7 @@
         at = (at - base).astype(F32)
 
         def body(s, carry):
-            value = table[s, m]
+            value = table[source_at(ps, s), batch_at(ps, s)]
             hi = value.astype(BF16)
             rest = value - hi.astype(F32)
             mid = rest.astype(BF16)
@@ -279,7 +296,7 @@
                 mixer[s, k * tok_n : (k + 1) * tok_n] = jnp.where(here, turn(v, spread_gate), 0.0).astype(BF16)
             return carry
 
-        lax.fori_loop(jnp.int32(0), jnp.int32(n_devs), body, 0)
+        lax.fori_loop(jnp.int32(0), jnp.int32(sources[ps]), body, 0)
 
     def r_pair(n):
         return remote(partial.at[1 - core], pair.at[n], pair_send.at[n], pair_recv.at[n], partner)
@@ -298,47 +315,70 @@
         )
 
     def out_copy(m, n):
-        return pltpu.make_async_copy(
-            out_stage.at[n], (out_a, out_b)[m].at[:, sl(n * cols, cols)], stage_sem.at[n]
-        )
-
-    def back_pair(n):
-        r_pair(n).start()
-
-    def back_far(n):
-        r_pair(n).wait()
-
-        def body(k, carry):
+        return pltpu.make_async_copy(out_stage.at[n], out.at[m, :, sl(n * cols, cols)], stage_sem.at[n])
+
+    def by_role(ps, ring, feeder):
+        if ps == 1:
+            ring()
+            feeder()
+        else:
+            on_core(ps // 2, ring)
+            on_core(1 - ps // 2, feeder)
+
+    def back_pair(ps, n):
+        by_role(ps, lambda: None, lambda: r_pair(n).start())
+
+    def back_far(ps, n):
+        def ring():
+            r_pair(n).wait_recv()
+
+            def body(k, carry):
+                for hf in range(2):
+                    pair[n, k, hf] += partial[core, k, hf]
+                return carry
+
+            lax.fori_loop(jnp.int32(0), jnp.int32(n_chips), body, 0)
+            for d in range(2):
+                r_far(n, d).start()
+            for d in range(2):
+                r_near(n, d, 1 - d).start()
+
+        by_role(ps, ring, lambda: r_pair(n).wait_send())
+
+    def back_near(ps, n):
+        def ring():
+            for d in range(2):
+                r_far(n, d).wait_recv()
+                pair[n, chip_side[d], d] += transit[n, d]
+                r_near(n, d, d).start()
+            own_rows(my_batch(ps), n).start()
+
+        by_role(ps, ring, lambda: None)
+
+    def back_out(ps, n):
+        def ring():
+            m = my_batch(ps)
+            for d in range(2):
+                r_far(n, d).wait_send()
+                for hf in range(2):
+                    r_near(n, d, hf).wait()
+            own_rows(m, n).wait()
+            if ps > 0:
+                @pl.when(m == 1)
+                def _():
+                    out_copy(0, n).wait()
             for hf in range(2):
-                pair[n, k, hf] += partial[core, k, hf]
-            return carry
-
-        lax.fori_loop(jnp.int32(0), jnp.int32(n_chips), body, 0)
-        for d in range(2):
-            r_far(n, d).start()
-        for d in range(2):
-            r_near(n, d, 1 - d).start()
-
-    def back_near(m, n):
-        for d in range(2):
-            r_far(n, d).wait_recv()
-            pair[n, chip_side[d], d] += transit[n, d]
-            r_near(n, d, d).start()
-        own_rows(m, n).start()
-
-    def back_out(m, n):
-        for d in range(2):
-            r_far(n, d).wait_send()
-            for hf in range(2):
-                r_near(n, d, hf).wait()
-        own_rows(m, n).wait()
-        if m == 1:
-            out_copy(0, n).wait()
-        for hf in range(2):
-            part = slice(hf * half, (hf + 1) * half)
-            total = pair[n, chip, hf] + near[n, 0, hf] + near[n, 1, hf]
-            out_stage[n, :, part] = (own_stage[n, :, part].astype(F32) + total).astype(BF16)
-        out_copy(m, n).start()
+                part = slice(hf * half, (hf + 1) * half)
+                total = pair[n, chip, hf] + near[n, 0, hf] + near[n, 1, hf]
+                out_stage[n, :, part] = (own_stage[n, :, part].astype(F32) + total).astype(BF16)
+            out_copy(m, n).start()
+
+        by_role(ps, ring, lambda: None)
+
+    def give_credit():
+        for dev in (right, left):
+            pl.semaphore_signal(ring_credit, inc=1, device_id={'ep': dev}, device_id_type=pl.DeviceIdType.MESH)
+        pl.semaphore_signal(pair_credit, inc=1, device_id={'ep': partner}, device_id_type=pl.DeviceIdType.MESH)
 
     for k in range(ahead):
         fetch_pair(0, k)
@@ -359,7 +399,7 @@
         to = rem(me + k, n_devs)
         return remote(meta.at[to], table.at[me], meta_send.at[k], meta_recv.at[k], to)
 
-    gather_start(0)
+    on_core(0, lambda: gather_start(0))
     n_experts = n_devs * local_n
     before = jnp.where(
         lax.broadcasted_iota(jnp.int32, (tok_n, tok_n), 0) < lax.broadcasted_iota(jnp.int32, (tok_n, tok_n), 1), 1.0, 0.0
@@ -425,7 +465,7 @@
 
         @pl.when(q == stream[1][2] // 2)
         def _():
-            gather_forward(0)
+            on_core(0, lambda: gather_forward(0))
 
         return carry
 
@@ -436,67 +476,78 @@
         qkv_copy(jnp.int32(j)).wait()
     for k in range(1, n_devs):
         m_send(k).wait()
-    make_mixer(0)
-    gather_pass(0)
-    gather_start(1)
-    gather_near_done(0)
-
-    for m in range(2):
-        dispatch(m, 0, n_devs - 2)
-        if m == 0:
-            gather_pass_far(0)
-            gather_done(0)
-        dispatch(m, n_devs - 2, n_devs)
-        if m == 1:
-            make_mixer(1)
-            back_far(jnp.int32(CHUNKS - 1))
-            back_near(0, jnp.int32(1))
-
-        def gu_expert(e, carry, m=m):
-            ph = 2 + 2 * m
+    on_core(0, lambda: gather_pass(0), lambda: gather_pass_far(0), lambda: gather_start(1))
+    on_core(1, lambda: gather_from_partner(0), lambda: gather_start(0))
+    i32 = jnp.int32
+    last = CHUNKS - 1
+
+    for ps in range(n_pass):
+        n_src = sources[ps]
+        taken = n_src * capacity
+        if ps == 1:
+            on_core(0, lambda: gather_from_partner(0))
+            on_core(1, lambda: gather_from_partner(1))
+        if ps == 2:
+            on_core(0, lambda: gather_from_partner(1), lambda: gather_sent(0), lambda: gather_sent(1))
+            on_core(1, lambda: gather_sent(0), lambda: gather_sent(1))
+        dispatch(ps)
+        if ps > 0:
+            back_far(ps - 1, i32(last))
+            back_near(ps - 1, i32(1))
+        make_mixer(ps)
+
+        gu_events = [
+            {
+                2: lambda: (on_core(0, lambda: gather_forward(1)), on_core(1, lambda: gather_forward(0))),
+                4: lambda: (
+                    on_core(0, lambda: gather_pass(1)),
+                    on_core(1, lambda: gather_pass(0), lambda: gather_start(1)),
+                ),
+            },
+            {
+                0: lambda: (back_near(0, i32(2)), on_core(1, lambda: gather_forward(1))),
+                1: lambda: (back_near(0, i32(3)), on_core(1, lambda: gather_pass(1))),
+                3: lambda: back_out(0, i32(0)),
+                4: lambda: (back_out(0, i32(1)), on_core(1, lambda: gather_pass_far(1))),
+                5: lambda: back_out(0, i32(2)),
+                6: lambda: (back_out(0, i32(3)), on_core(0, give_credit)),
+            },
+            {
+                1: lambda: back_near(1, i32(2)),
+                3: lambda: back_out(1, i32(0)),
+                4: lambda: back_near(1, i32(3)),
+                5: lambda: back_out(1, i32(1)),
+                6: lambda: back_out(1, i32(2)),
+            },
+        ][ps]
+
+        def gu_expert(e, carry, ps=ps, taken=taken, gu_events=gu_events):
+            ph = 2 + 2 * ps
             for r in range(gu_pairs):
                 arrive(ph, e, r)
                 next_pair_gu(ph, e, r)
                 slot = slot_of(ph, e * gu_pairs + r)
                 for k in range(2):
                     t = 2 * r + k
+                    x = rows[e, 0:taken]
                     if t < n_full:
-                        g = jnp.dot(rows[e], wbuf[slot, k, :, 0:WIDE], preferred_element_type=F32)
-                        u = jnp.dot(rows[e], wbuf[slot, k, :, WIDE : 2 * WIDE], preferred_element_type=F32)
-                        hidden[e, :, t * WIDE : (t + 1) * WIDE] = (jax.nn.silu(g) * u).astype(BF16)
+                        g = jnp.dot(x, wbuf[slot, k, :, 0:WIDE], preferred_element_type=F32)
+                        u = jnp.dot(x, wbuf[slot, k, :, WIDE : 2 * WIDE], preferred_element_type=F32)
+                        hidden[e, 0:taken, t * WIDE : (t + 1) * WIDE] = (jax.nn.silu(g) * u).astype(BF16)
                     else:
-                        gu = jnp.dot(rows[e], wbuf[slot, k, :, 0 : 2 * tail], preferred_element_type=F32)
-                        hidden[e, :, n_full * WIDE : ff] = (
+                        gu = jnp.dot(x, wbuf[slot, k, :, 0 : 2 * tail], preferred_element_type=F32)
+                        hidden[e, 0:taken, n_full * WIDE : ff] = (
                             jax.nn.silu(gu[:, 0:tail]) * gu[:, tail : 2 * tail]
                         ).astype(BF16)
-
-            if m == 0:
-                events = {2: [lambda: gather_forward(1)], 4: [lambda: gather_pass(1)]}
-            else:
-                events = {
-                    1: [lambda: back_near(0, jnp.int32(2))],
-                    3: [lambda: back_out(0, jnp.int32(0))],
-                    4: [lambda: back_near(0, jnp.int32(3))],
-                    5: [lambda: back_out(0, jnp.int32(1))],
-                    6: [lambda: back_out(0, jnp.int32(2))],
-                    7: [lambda: back_out(0, jnp.int32(3))],
-                }
-            for at, steps in events.items():
-                def run(steps=steps):
-                    for step in steps:
-                        step()
-                pl.when(e == at)(run)
+            for at, step in gu_events.items():
+                pl.when(e == at)(lambda step=step: (step(), None)[1])
             return carry
 
-        lax.fori_loop(jnp.int32(0), jnp.int32(local_n), gu_expert, 0)
-        if m == 0:
-            gather_pass_far(1)
-        else:
-            for dev in (partner, right, left):
-                pl.semaphore_signal(credit, inc=1, device_id={'ep': dev}, device_id_type=pl.DeviceIdType.MESH)
-
-        def down_chunk(n, carry, m=m):
-            ph = 3 + 2 * m
+        lax.fori_loop(i32(0), i32(local_n), gu_expert, 0)
+
+        def down_chunk(n, carry, ps=ps, n_src=n_src, taken=taken):
+            ph = 3 + 2 * ps
+            final = local_n // 2 - 1
 
             def pair_of(r, carry):
                 q = n * (local_n // 2) + r
@@ -505,60 +556,73 @@
                 slot = slot_of(ph, q)
                 for k in range(2):
                     e = 2 * r + k
-                    y = jnp.dot(hidden[e], wbuf[slot, k, 0:ff, 0:cols], preferred_element_type=F32).astype(BF16)
-                    expert_out[:, pl.ds(pl.multiple_of(e * capacity, capacity), capacity), :] = y.reshape(
-                        n_devs, capacity, cols
+                    y = jnp.dot(hidden[e, 0:taken], wbuf[slot, k, 0:ff, 0:cols], preferred_element_type=F32)
+                    expert_out[0:n_src, pl.ds(pl.multiple_of(e * capacity, capacity), capacity), :] = (
+                        y.astype(BF16).reshape(n_src, capacity, cols)
                     )
 
-                @pl.when((r == 1) & (n == 2))
+                if ps == 0:
+                    @pl.when((r == final) & (n == 0))
+                    def _():
+                        on_core(0, lambda: gather_pass_far(1))
+                        on_core(1, lambda: gather_pass_far(0))
+
+                if ps == 2:
+                    @pl.when((r == 1) & (n == 0))
+                    def _():
+                        back_out(1, i32(last))
+                        on_core(1, give_credit)
+
+                @pl.when((r == final) & (n == 2))
                 def _():
-                    back_near(m, jnp.int32(0))
-
-                @pl.when((r == 2) & (n >= 1))
+                    back_near(ps, i32(0))
+
+                @pl.when((r == (final - 1 if ps == 1 else final)) & (n >= 1))
                 def _():
-                    back_far(n - 1)
+                    back_far(ps, n - 1)
 
                 return carry
 
-            lax.fori_loop(jnp.int32(0), jnp.int32(local_n // 2), pair_of, 0)
+            lax.fori_loop(i32(0), i32(local_n // 2), pair_of, 0)
 
             def mix(r, carry):
                 for k in range(2):
+                    t = 2 * r + k
                     for hf in range(2):
-                        ys = expert_out[2 * r + k, :, hf * half : (hf + 1) * half]
-                        got = jnp.dot(mixer[2 * r + k], ys, preferred_element_type=F32)
-                        partial[k, r, hf] = got[0:tok_n] + got[tok_n : 2 * tok_n] + got[2 * tok_n : 3 * tok_n]
+                        ys = expert_out[t, :, hf * half : (hf + 1) * half]
+                        got = jnp.dot(mixer[t], ys, preferred_element_type=F32)
+                        partial[core_at(ps, t), rem(t, n_chips), hf] = (
+                            got[0:tok_n] + got[tok_n : 2 * tok_n] + got[2 * tok_n : 3 * tok_n]
+                        )
                 return carry
 
-            lax.fori_loop(jnp.int32(0), jnp.int32(n_devs // 2), mix, 0)
-            if m == 1:
+            lax.fori_loop(i32(0), i32(n_src // 2), mix, 0)
+            if ps > 0:
                 @pl.when(n == 0)
                 def _():
-                    pl.semaphore_wait(credit, 3)
-
-            back_pair(n)
+                    on_core(ps - 1, lambda: pl.semaphore_wait(ring_credit, 2))
+                    on_core(2 - ps, lambda: pl.semaphore_wait(pair_credit, 1))
+
+            back_pair(ps, n)
             return carry
 
-        lax.fori_loop(jnp.int32(0), jnp.int32(CHUNKS), down_chunk, 0)
-        if m == 0:
-            gather_near_done(1)
-            gather_done(1)
-
-    back_near(1, jnp.int32(1))
-    back_far(jnp.int32(CHUNKS - 1))
-    back_near(1, jnp.int32(2))
-    back_out(1, jnp.int32(0))
-    back_near(1, jnp.int32(3))
+        lax.fori_loop(i32(0), i32(CHUNKS), down_chunk, 0)
+
+    back_far(2, i32(last))
+    back_near(2, i32(1))
+    back_near(2, i32(2))
+    back_out(2, i32(0))
+    back_near(2, i32(3))
     for n in range(1, CHUNKS):
-        back_out(1, jnp.int32(n))
+        back_out(2, i32(n))
     for n in range(CHUNKS):
-        out_copy(1, jnp.int32(n)).wait()
-
-
-def hand_over_kernel(*refs):
-    ins, outs, bufs, sems = refs[0:3], refs[3:6], refs[6:9], refs[9]
+        out_copy(1, i32(n)).wait()
+
+
+def hand_over_kernel(both, qkv, out_a, out_b, out_qkv, *scratch):
+    ins, outs, bufs, sems = (both.at[0], both.at[1], qkv), (out_a, out_b, out_qkv), scratch[0:3], scratch[3]
     pieces = sems.shape[2]
-    size = ins[0].shape[0] // pieces
+    size = qkv.shape[0] // pieces
 
     def move(src, dst, i, p, way):
         at = pl.ds(p * size, size)
@@ -574,17 +638,18 @@
         move(bufs[i], outs[i], i, p, 1).wait()
 
 
-def hand_over(arrays):
+def hand_over(both, qkv):
     any_spec = pl.BlockSpec(memory_space=pl.ANY)
+    results = [jax.ShapeDtypeStruct(both.shape[1:], both.dtype)] * 2 + [jax.ShapeDtypeStruct(qkv.shape, qkv.dtype)]
     return pl.pallas_call(
         hand_over_kernel,
-        in_specs=[any_spec] * 3,
+        in_specs=[any_spec] * 2,
         out_specs=[any_spec] * 3,
-        out_shape=[jax.ShapeDtypeStruct(a.shape, a.dtype) for a in arrays],
-        scratch_shapes=[pltpu.VMEM(a.shape, a.dtype) for a in arrays] + [pltpu.SemaphoreType.DMA((2, 3, 4))],
+        out_shape=results,
+        scratch_shapes=[pltpu.VMEM(a.shape, a.dtype) for a in results] + [pltpu.SemaphoreType.DMA((2, 3, 4))],
         compiler_params=pltpu.CompilerParams(vmem_limit_bytes=VMEM_LIMIT),
         name="hand_over",
-    )(*arrays)
+    )(both, qkv)
 
 
 def solution(mesh):
@@ -606,13 +671,12 @@
             moe_kernel(capacity, *refs)
 
         flops = 2 * (6 * local_n * row_n * dim * ff + 8 * n_devs * n_slots * tok_n * dim) + 2 * tok_n * dim * 4 * dim
-        out_a, out_b, qkv_b, _ = pl.pallas_call(
+        both, qkv_b, _ = pl.pallas_call(
             body,
             in_specs=[any_spec] * 3 + [pl.BlockSpec(memory_space=pltpu.VMEM)] * 4 + [any_spec] * 5,
-            out_specs=[any_spec] * 4,
+            out_specs=[any_spec] * 3,
             out_shape=[
-                jax.ShapeDtypeStruct((tok_n, dim), BF16),
-                jax.ShapeDtypeStruct((tok_n, dim), BF16),
+                jax.ShapeDtypeStruct((2, tok_n, dim), BF16),
                 jax.ShapeDtypeStruct((tok_n, w_qkv.shape[1]), BF16),
                 jax.ShapeDtypeStruct((2, n_devs, tok_n, dim), BF16),
             ],
@@ -645,6 +709,7 @@
                 dma((CHUNKS, 2, 2)),
                 dma((CHUNKS, 2, 2)),
                 pltpu.SemaphoreType.REGULAR,
+                pltpu.SemaphoreType.REGULAR,
             ],
             compiler_params=pltpu.CompilerParams(
                 collective_id=0, has_side_effects=True, vmem_limit_bytes=VMEM_LIMIT
@@ -652,7 +717,7 @@
             cost_estimate=pl.CostEstimate(flops=flops, bytes_accessed=400_000_000, transcendentals=0),
             name="moe_step",
         )(x_a, h_b, attn_b, route_a.T, gate_a.T, route_b.T, gate_b.T, w_qkv, w_o, w_gate, w_up, w_down)
-        return tuple(hand_over((out_a, out_b, qkv_b)))
+        return tuple(hand_over(both, qkv_b))
 
     row_spec = P(('dp', 'ep'), None)
     full_spec = P(None, None)

time: 289 us -> 286 us (0.990)
  Pallas kernels: 288 us -> 284 us
    pallas_call x1, Pallas kernels: 283 us -> 280 us  [local_step(): pl.pallas_call(body, in_specs=[any_spec] * 3 + [pl.BlockSpec(memory_space...]
where the time goes in v4:
time: 286 us; the launch traced here: 285 us
  Pallas kernels  284 us (99%)
    pallas_call x1, Pallas kernels, local_step(): pl.pallas_call(body, in_specs=[any_spec] * 3 + [pl.BlockSpec(memory_space...  280 us

profile of v4, /device:TPU:81, one launch (start us, length us, event | category | flops | bytes accessed | tf_op | source)
XLA Modules:
  0.0 285.2 jit_solution(16827502737131449932)
XLA Ops:
  0.6 279.5 %moe_step.1 = (bf16[2,256,2048]{2,1,0:T(8,128)(2,1)}, bf16[256,6144]{1,0:T(8,128)(2,1)}, bf16[2,8,256,2048]{3,2,1,0:T(8,128)(2,1)}) custom-call(bf16[256,2048]{1,0:T(8,128)(2,1)} %refs_0_.1, bf16[256,2048]{1,0:T(8,128)(2,1)} %refs_1_.1, bf16[256,2048]{1,0:T(8,128)(2,1)} %refs_2_.1, s32[6,256]{1,0:T(8,128)} %bitcast.4, f32[6,256]{1,0:T(8,128)} %bitcast.5, ...), custom_call_target="tpu_custom_call" | custom-call | flops 140660178944 | bytes 400000000 | tf_op jit(solution)/shard_map/moe_step/pallas_call | solution.py:674
  280.1 4.9 %hand_over.1 = (bf16[256,2048]{1,0:T(8,128)(2,1)}, bf16[256,2048]{1,0:T(8,128)(2,1)}, bf16[256,6144]{1,0:T(8,128)(2,1)}) custom-call(bf16[2,256,2048]{2,1,0:T(8,128)(2,1)} %get-tuple-element.5.both, bf16[256,6144]{1,0:T(8,128)(2,1)} %get-tuple-element.6.qkv), custom_call_target="tpu_custom_call" | custom-call | tf_op jit(solution)/shard_map/hand_over/pallas_call | solution.py:644

commit v5 on v4

--- a/solution.py
+++ b/solution.py
@@ -25,7 +25,7 @@
     capacity,
     x_a, h_b, attn_b, route_a, gate_a, route_b, gate_b, w_qkv, w_o, w_gate, w_up, w_down,
     out, qkv, land,
-    wbuf, rows, hidden, meta, expert_out, mixer, partial, pair, transit, near, out_stage, own_stage, table,
+    wbuf, rows, hidden, meta, src_rows, mixer, partial, pair, transit, near, out_stage, own_stage, table,
     w_sem, gather_send, gather_recv, meta_send, meta_recv, load_sem, stage_sem, own_sem,
     pair_send, pair_recv, far_send, far_recv, near_send, near_recv, ring_credit, pair_credit,
 ):
@@ -79,7 +79,7 @@
                 w = w_o if kind == 'proj' else w_qkv
                 out.append((w.at[:, sl((2 * q + k) * cols, cols)], buf.at[:, 0:cols], sem.at[0]))
             elif kind == 'down':
-                n, e = div(q, local_n // 2), rem(q, local_n // 2) * 2 + k
+                e, n = div(q, CHUNKS // 2), rem(q, CHUNKS // 2) * 2 + k
                 out.append((w_down.at[e, :, sl(n * cols, cols)], buf.at[0:ff, 0:cols], sem.at[0]))
             else:
                 t = 2 * r + k
@@ -219,24 +219,9 @@
     def my_batch(ps):
         return 1 - core if ps == 1 else jnp.int32(ps // 2)
 
-    class load:
-        def __init__(self, ps, k):
-            self.copies = [
-                pltpu.make_async_copy(
-                    land.at[batch_at(ps, k), source_at(ps, k), :, j * cols : (j + 1) * cols],
-                    expert_out.at[CHUNKS * rem(k, 2) + j, 0:tok_n],
-                    load_sem.at[rem(k, 2), j],
-                )
-                for j in range(CHUNKS)
-            ]
-
-        def start(self):
-            for c in self.copies:
-                c.start()
-
-        def wait(self):
-            for c in self.copies:
-                c.wait()
+    def load(ps, k):
+        slot = rem(k, 2)
+        return pltpu.make_async_copy(land.at[batch_at(ps, k), source_at(ps, k)], src_rows.at[slot], load_sem.at[slot])
 
     def dispatch(ps):
         hi = sources[ps]
@@ -256,7 +241,7 @@
             )
             for j in range(CHUNKS):
                 part = slice(j * cols, (j + 1) * cols)
-                got = jnp.dot(pick, expert_out[CHUNKS * slot + j, 0:tok_n], preferred_element_type=F32).astype(BF16)
+                got = jnp.dot(pick, src_rows[slot, :, part], preferred_element_type=F32).astype(BF16)
                 for e in range(local_n):
                     rows[e, pl.ds(pl.multiple_of(k * capacity, capacity), capacity), part] = got[
                         e * capacity : (e + 1) * capacity
@@ -299,7 +284,7 @@
         lax.fori_loop(jnp.int32(0), jnp.int32(sources[ps]), body, 0)
 
     def r_pair(n):
-        return remote(partial.at[1 - core], pair.at[n], pair_send.at[n], pair_recv.at[n], partner)
+        return remote(partial.at[1 + rem(n, 2)], pair.at[n], pair_send.at[n], pair_recv.at[n], partner)
 
     def r_far(n, d):
         return remote(pair.at[n, chip_far, d], transit.at[n, d], far_send.at[n, d], far_recv.at[n, d], sides[d])
@@ -334,7 +319,7 @@
 
             def body(k, carry):
                 for hf in range(2):
-                    pair[n, k, hf] += partial[core, k, hf]
+                    pair[n, k, hf] += partial[0, k, hf]
                 return carry
 
             lax.fori_loop(jnp.int32(0), jnp.int32(n_chips), body, 0)
@@ -343,7 +328,10 @@
             for d in range(2):
                 r_near(n, d, 1 - d).start()
 
-        by_role(ps, ring, lambda: r_pair(n).wait_send())
+        by_role(ps, ring, lambda: None)
+
+    def back_given(ps, n):
+        by_role(ps, lambda: None, lambda: r_pair(n).wait_send())
 
     def back_near(ps, n):
         def ring():
@@ -387,8 +375,8 @@
         pl.semaphore_signal(
             barrier, inc=1, device_id={'ep': rem(me + k, n_devs)}, device_id_type=pl.DeviceIdType.MESH
         )
-    attn_in = pltpu.make_async_copy(attn_b, rows.at[0, 0:tok_n], load_sem.at[0, 0])
-    h_in = pltpu.make_async_copy(h_b, rows.at[1, 0:tok_n], load_sem.at[1, 0])
+    attn_in = pltpu.make_async_copy(attn_b, rows.at[0, 0:tok_n], load_sem.at[0])
+    h_in = pltpu.make_async_copy(h_b, rows.at[1, 0:tok_n], load_sem.at[1])
     x_in = pltpu.make_async_copy(x_a, rows.at[3, 0:tok_n], own_sem.at[0])
     attn_in.start()
     h_in.start()
@@ -493,7 +481,8 @@
         dispatch(ps)
         if ps > 0:
             back_far(ps - 1, i32(last))
-            back_near(ps - 1, i32(1))
+        if ps == 1:
+            back_near(0, i32(0))
         make_mixer(ps)
 
         gu_events = [
@@ -505,19 +494,19 @@
                 ),
             },
             {
-                0: lambda: (back_near(0, i32(2)), on_core(1, lambda: gather_forward(1))),
-                1: lambda: (back_near(0, i32(3)), on_core(1, lambda: gather_pass(1))),
+                0: lambda: (back_near(0, i32(1)), on_core(1, lambda: gather_forward(1))),
+                1: lambda: (back_near(0, i32(2)), on_core(1, lambda: gather_pass(1))),
+                2: lambda: back_near(0, i32(3)),
                 3: lambda: back_out(0, i32(0)),
                 4: lambda: (back_out(0, i32(1)), on_core(1, lambda: gather_pass_far(1))),
                 5: lambda: back_out(0, i32(2)),
                 6: lambda: (back_out(0, i32(3)), on_core(0, give_credit)),
             },
             {
-                1: lambda: back_near(1, i32(2)),
-                3: lambda: back_out(1, i32(0)),
-                4: lambda: back_near(1, i32(3)),
-                5: lambda: back_out(1, i32(1)),
-                6: lambda: back_out(1, i32(2)),
+                0: lambda: back_near(1, i32(1)),
+                3: lambda: back_near(1, i32(2)),
+                5: lambda: back_out(1, i32(0)),
+                7: lambda: back_near(1, i32(3)),
             },
         ][ps]
 
@@ -545,70 +534,84 @@
 
         lax.fori_loop(i32(0), i32(local_n), gu_expert, 0)
 
-        def down_chunk(n, carry, ps=ps, n_src=n_src, taken=taken):
+        def down_pair(q, carry, ps=ps, taken=taken):
             ph = 3 + 2 * ps
-            final = local_n // 2 - 1
-
-            def pair_of(r, carry):
-                q = n * (local_n // 2) + r
-                arrive(ph, q)
-                next_pair(ph, q)
-                slot = slot_of(ph, q)
-                for k in range(2):
-                    e = 2 * r + k
-                    y = jnp.dot(hidden[e, 0:taken], wbuf[slot, k, 0:ff, 0:cols], preferred_element_type=F32)
-                    expert_out[0:n_src, pl.ds(pl.multiple_of(e * capacity, capacity), capacity), :] = (
-                        y.astype(BF16).reshape(n_src, capacity, cols)
-                    )
-
-                if ps == 0:
-                    @pl.when((r == final) & (n == 0))
-                    def _():
-                        on_core(0, lambda: gather_pass_far(1))
-                        on_core(1, lambda: gather_pass_far(0))
-
-                if ps == 2:
-                    @pl.when((r == 1) & (n == 0))
-                    def _():
-                        back_out(1, i32(last))
-                        on_core(1, give_credit)
-
-                @pl.when((r == final) & (n == 2))
+            arrive(ph, q)
+            next_pair(ph, q)
+            slot = slot_of(ph, q)
+            e, first = div(q, CHUNKS // 2), rem(q, CHUNKS // 2) * 2
+            for k in range(2):
+                y = jnp.dot(hidden[e, 0:taken], wbuf[slot, k, 0:ff, 0:cols], preferred_element_type=F32)
+                rows[e, 0:taken, sl((first + k) * cols, cols)] = y.astype(BF16)
+
+            if ps == 0:
+                @pl.when(q == 3)
                 def _():
-                    back_near(ps, i32(0))
-
-                @pl.when((r == (final - 1 if ps == 1 else final)) & (n >= 1))
+                    on_core(0, lambda: gather_pass_far(1))
+                    on_core(1, lambda: gather_pass_far(0))
+
+            if ps == 2:
+                for at, n in ((2, 1), (6, 2)):
+                    @pl.when(q == at)
+                    def _(n=n):
+                        back_out(1, i32(n))
+
+            return carry
+
+        lax.fori_loop(i32(0), i32(CHUNKS // 2 * local_n), down_pair, 0)
+        if ps == 2:
+            back_out(1, i32(last))
+            on_core(1, give_credit)
+        if ps > 0:
+            on_core(ps - 1, lambda: pl.semaphore_wait(ring_credit, 2))
+            on_core(2 - ps, lambda: pl.semaphore_wait(pair_credit, 1))
+
+        def mix_chunk(n, carry, ps=ps, n_src=n_src):
+            def mix(lo, where):
+                def body(r, carry):
+                    for k in range(2):
+                        t = rem(lo + 2 * r + k, n_src)
+                        here = pl.ds(pl.multiple_of(t * capacity, capacity), capacity)
+                        for hf in range(2):
+                            at = sl(n * cols + hf * half, half)
+                            ys = jnp.concatenate([rows[e, here, at] for e in range(local_n)], axis=0)
+                            got = jnp.dot(mixer[t], ys, preferred_element_type=F32)
+                            partial[where, rem(t, n_chips), hf] = (
+                                got[0:tok_n] + got[tok_n : 2 * tok_n] + got[2 * tok_n : 3 * tok_n]
+                            )
+                    return carry
+
+                lax.fori_loop(i32(0), i32(n_chips // 2), body, 0)
+
+            @pl.when(n >= 2)
+            def _():
+                back_given(ps, n - 2)
+
+            def follow():
+                @pl.when(n >= 1)
                 def _():
                     back_far(ps, n - 1)
 
-                return carry
-
-            lax.fori_loop(i32(0), i32(local_n // 2), pair_of, 0)
-
-            def mix(r, carry):
-                for k in range(2):
-                    t = 2 * r + k
-                    for hf in range(2):
-                        ys = expert_out[t, :, hf * half : (hf + 1) * half]
-                        got = jnp.dot(mixer[t], ys, preferred_element_type=F32)
-                        partial[core_at(ps, t), rem(t, n_chips), hf] = (
-                            got[0:tok_n] + got[tok_n : 2 * tok_n] + got[2 * tok_n : 3 * tok_n]
-                        )
-                return carry
-
-            lax.fori_loop(i32(0), i32(n_src // 2), mix, 0)
-            if ps > 0:
-                @pl.when(n == 0)
-                def _():
-                    on_core(ps - 1, lambda: pl.semaphore_wait(ring_credit, 2))
-                    on_core(2 - ps, lambda: pl.semaphore_wait(pair_credit, 1))
-
-            back_pair(ps, n)
+            if ps == 1:
+                mix(n_chips * core, 1 + rem(n, 2))
+                back_pair(ps, n)
+                follow()
+                mix(n_chips * (1 - core), 0)
+            else:
+                follow()
+                mine = 1 - (ps // 2 - core) * (ps // 2 - core)
+                mix(i32(0), (1 - mine) * (1 + rem(n, 2)))
+                back_pair(ps, n)
             return carry
 
-        lax.fori_loop(i32(0), i32(CHUNKS), down_chunk, 0)
+        lax.fori_loop(i32(0), i32(CHUNKS), mix_chunk, 0)
+        for n in range(CHUNKS - 2, CHUNKS):
+            back_given(ps, i32(n))
+        if ps == 1:
+            back_near(ps, i32(0))
 
     back_far(2, i32(last))
+    back_near(2, i32(0))
     back_near(2, i32(1))
     back_near(2, i32(2))
     back_out(2, i32(0))
@@ -685,9 +688,9 @@
                 pltpu.VMEM((local_n, row_n, dim), BF16),
                 pltpu.VMEM((local_n, row_n, ff), BF16),
                 pltpu.VMEM((n_devs, 2, 2 * local_n, tok_n), F32),
-                pltpu.VMEM((n_devs, n_slots, cols), BF16),
+                pltpu.VMEM((2, tok_n, dim), BF16),
                 pltpu.VMEM((n_devs, 3 * tok_n, n_slots), BF16),
-                pltpu.VMEM((2, n_chips, 2, tok_n, half), F32),
+                pltpu.VMEM((3, n_chips, 2, tok_n, half), F32),
                 pltpu.VMEM((CHUNKS, n_chips, 2, tok_n, half), F32),
                 pltpu.VMEM((CHUNKS, 2, tok_n, half), F32),
                 pltpu.VMEM((CHUNKS, 2, 2, tok_n, half), F32),
@@ -699,7 +702,7 @@
                 dma((2, 11)),
                 dma((n_devs,)),
                 dma((n_devs,)),
-                dma((2, CHUNKS)),
+                dma((2,)),
                 dma((CHUNKS,)),
                 dma((CHUNKS,)),
                 dma((CHUNKS,)),

time: 286 us -> 307 us (1.073)
  Pallas kernels: 284 us -> 306 us
    pallas_call x1, Pallas kernels: 280 us -> 301 us  [local_step(): pl.pallas_call(body, in_specs=[any_spec] * 3 + [pl.BlockSpec(memory_space...]
where the time goes in v5:
time: 307 us
  Pallas kernels  306 us (100%)
    pallas_call x1, Pallas kernels, local_step(): pl.pallas_call(body, in_specs=[any_spec] * 3 + [pl.BlockSpec(memory_space...  301 us

profile of v5, /device:TPU:81, one launch (start us, length us, event | category | flops | bytes accessed | tf_op | source)
XLA Modules:
  0.0 307.0 jit_solution(1879621695775034326)
XLA Ops:
  0.6 301.3 %moe_step.1 = (bf16[2,256,2048]{2,1,0:T(8,128)(2,1)}, bf16[256,6144]{1,0:T(8,128)(2,1)}, bf16[2,8,256,2048]{3,2,1,0:T(8,128)(2,1)}) custom-call(bf16[256,2048]{1,0:T(8,128)(2,1)} %refs_0_.1, bf16[256,2048]{1,0:T(8,128)(2,1)} %refs_1_.1, bf16[256,2048]{1,0:T(8,128)(2,1)} %refs_2_.1, s32[6,256]{1,0:T(8,128)} %bitcast.4, f32[6,256]{1,0:T(8,128)} %bitcast.5, ...), custom_call_target="tpu_custom_call" | custom-call | flops 140660178944 | bytes 400000000 | tf_op jit(solution)/shard_map/moe_step/pallas_call | solution.py:677
  302.0 4.9 %hand_over.1 = (bf16[256,2048]{1,0:T(8,128)(2,1)}, bf16[256,2048]{1,0:T(8,128)(2,1)}, bf16[256,6144]{1,0:T(8,128)(2,1)}) custom-call(bf16[2,256,2048]{2,1,0:T(8,128)(2,1)} %get-tuple-element.5.both, bf16[256,6144]{1,0:T(8,128)(2,1)} %get-tuple-element.6.qkv), custom_call_target="tpu_custom_call" | custom-call | tf_op jit(solution)/shard_map/hand_over/pallas_call | solution.py:647
